TPU v7x, 32 devices: a whole 2x2x4 slice. The times are simulated.
32 devices in a mesh: group: 2 (over x), lat: 16 (over z, y, core).
Axes of the slice: x: 2, y: 2, z: 4, core: 2. Of those that a mesh axis runs over, the one named last changes fastest.
Arguments:
- grid_values: bfloat16 [224, 1440, 256], P(('group', 'lat')), parts along dimension 0, may hold values from -630 to 630
- lat_counts: int32 [16], replicated, may hold values from 1 to 7, 96 in all
- owner_wavenumber: int32 [384], replicated, may hold values from 0 to 383, each once
- legendre: bfloat16 [384, 96, 384], P('lat'), may hold values from -0.625 to 0.625
- quad_weight: float32 [96], replicated, may hold values from 0.3 to 3
- spectral_gain: float32 [384, 256], replicated, may hold values from 0.3 to 3
- channel_mix: bfloat16 [256, 256], replicated, may hold values from -0.375 to 0.375
Outputs:
- grid_output: bfloat16 [224, 1440, 256], P(('group', 'lat')), parts along dimension 0
There are 2 independent parts, one for each index of `group`. A program takes and returns all parts, laid end to end along the dimension named above; an argument that names none is the same for every part. Nothing has to cross between parts.
Inputs may be any that keep to these rules, and one draw needn't show every extreme that they name: `lat_counts`: some device has all 7 slots live. `owner_wavenumber`: each wavenumber appears once; device i of lat owns wavenumber slots i * 24 to (i + 1) * 24 - 1.
All inputs are finite; a program needn't handle non-finite values.
Results may differ from a plain program's by a relative error of at most 0.0095.
Values may be sent and summed in bfloat16 or wider, within the bound.
No kernel may reach another device: no remote copies, remote signals or barrier semaphores. Data moves between devices by JAX's collectives and lax.ppermute only.
A program may use at most 64 MiB of HBM per device.

v0:
```python
import math

import jax
import jax.numpy as jnp
from jax import lax
from jax.sharding import PartitionSpec as P


def live_slots(lat_counts, slot_count, live_total):
    devices = lat_counts.shape[0]
    starts = jnp.cumsum(lat_counts) - lat_counts
    device_ids = jnp.arange(devices, dtype=jnp.int32)
    slot_ids = jnp.arange(devices * slot_count, dtype=jnp.int32)
    holder = slot_ids // slot_count
    within = slot_ids - holder * slot_count
    holder_hot = holder[:, None] == device_ids[None, :]
    holder_count = jnp.sum(jnp.where(holder_hot, lat_counts[None, :], 0), axis=1)
    holder_start = jnp.sum(jnp.where(holder_hot, starts[None, :], 0), axis=1)
    slot_valid = within < holder_count
    slot_live = jnp.where(slot_valid, holder_start + within, 0)
    live_ids = jnp.arange(live_total, dtype=jnp.int32)
    reached = (starts[None, :] <= live_ids[:, None]).astype(jnp.int32)
    source = jnp.sum(reached, axis=1) - 1
    source_hot = source[:, None] == device_ids[None, :]
    source_start = jnp.sum(jnp.where(source_hot, starts[None, :], 0), axis=1)
    live_slot = source * slot_count + live_ids - source_start
    return (slot_valid, slot_live, live_slot)


def wave_angles(wave_list, longitudes):
    points = jnp.arange(longitudes, dtype=jnp.int32)
    phase = wave_list[:, None] * points[None, :] % longitudes
    return phase.astype(jnp.float32) * (2.0 * math.pi / longitudes)


def forward_table(wave_list, longitudes):
    angle = wave_angles(wave_list, longitudes)
    factor = 1.0 / math.sqrt(longitudes)
    return jnp.stack([jnp.cos(angle) * factor, -jnp.sin(angle) * factor], axis=1).astype(
        jnp.bfloat16
    )


def inverse_table(wave_list, longitudes):
    angle = wave_angles(wave_list, longitudes)
    factor = 1.0 / math.sqrt(longitudes)
    doubled = jnp.where(wave_list > 0, 2.0, 1.0).astype(jnp.float32)[:, None] * factor
    return jnp.stack([jnp.cos(angle) * doubled, -jnp.sin(angle) * doubled], axis=1).astype(
        jnp.bfloat16
    )


def body(
    grid_values, lat_counts, owner_wavenumber, legendre, quad_weight, spectral_gain, channel_mix
):
    slot_count, longitudes, channels = grid_values.shape
    my_index = lax.axis_index("lat")
    wave_count = owner_wavenumber.shape[0]
    wave_share, live_total, degrees = legendre.shape
    slot_valid, slot_live, live_slot = live_slots(lat_counts, slot_count, live_total)
    local_valid = lax.dynamic_slice_in_dim(slot_valid, my_index * slot_count, slot_count)
    row_weight = local_valid.astype(jnp.float32)[:, None, None]
    widened = grid_values.astype(jnp.float32) * row_weight
    totals = lax.psum(
        (jnp.sum(widened, axis=(0, 1)), jnp.sum(widened * widened, axis=(0, 1))), "lat"
    )
    points = live_total * longitudes
    channel_mean = totals[0] / points
    variance = totals[1] / points - channel_mean * channel_mean
    normed = (
        (grid_values.astype(jnp.float32) - channel_mean) * lax.rsqrt(variance + 1e-05) * row_weight
    ).astype(jnp.bfloat16)
    forward_flat = forward_table(owner_wavenumber, longitudes).reshape(2 * wave_count, longitudes)
    spectra = jnp.einsum("skc,qk->sqc", normed, forward_flat, preferred_element_type=jnp.float32)
    spectra = spectra.astype(jnp.bfloat16).reshape(slot_count, wave_count, 2, normed.shape[2])
    received = lax.all_to_all(spectra, "lat", split_axis=1, concat_axis=0, tiled=True)
    own_waves = lax.dynamic_slice_in_dim(owner_wavenumber, my_index * wave_share, wave_share)
    degree_mask = (jnp.arange(degrees, dtype=jnp.int32)[None, :] >= own_waves[:, None]).astype(
        jnp.float32
    )
    gathered = jnp.take(received, live_slot, axis=0)
    weighted = (gathered.astype(jnp.float32) * quad_weight[:, None, None, None]).astype(
        jnp.bfloat16
    )
    coefficient = jnp.einsum(
        "rgl,grtc->rltc", legendre, weighted, preferred_element_type=jnp.float32
    )
    filtered = (
        coefficient * degree_mask[:, :, None, None] * spectral_gain[None, :, None, :]
    ).astype(jnp.bfloat16)
    mixed = jnp.dot(filtered.reshape(-1, channels), channel_mix, preferred_element_type=jnp.float32)
    mixed = mixed.astype(jnp.bfloat16).reshape(wave_share, degrees, 2, channels)
    synthesis = jnp.einsum(
        "rgl,rltc->grtc", legendre, mixed, preferred_element_type=jnp.float32
    ).astype(jnp.bfloat16)
    outgoing = jnp.where(
        slot_valid[:, None, None, None],
        jnp.take(synthesis, slot_live, axis=0),
        jnp.zeros((), jnp.bfloat16),
    )
    inverse_flat = inverse_table(owner_wavenumber, longitudes).reshape(2 * wave_count, longitudes)
    returned = lax.all_to_all(outgoing, "lat", split_axis=0, concat_axis=1, tiled=True)
    flat_back = returned.reshape(slot_count, 2 * wave_count, returned.shape[3])
    return jnp.einsum(
        "sqc,qk->skc", flat_back, inverse_flat, preferred_element_type=jnp.float32
    ).astype(jnp.bfloat16)


def solution(mesh):
    return jax.shard_map(
        body,
        mesh=mesh,
        in_specs=(P(("group", "lat"), None, None), P(), P(), P("lat", None, None), P(), P(), P()),
        out_specs=P(("group", "lat"), None, None),
        check_vma=False,
    )
```

profile of v0, /device:TPU:15, one launch (start us, length us, event | category | flops | bytes accessed | tf_op | source)
XLA Modules:
  0.0 337.3 jit_solution(7146616504685830470)
XLA Ops:
  0.0 0.0 copy-start
  0.0 0.9 copy.57
  0.9 0.1 reduce
  1.0 0.7 sub.72
  1.7 0.7 select_multiply_fusion
  2.4 10.7 %multiply_convert_fusion.4 = (bf16[384,1,1440]{0,2,1:T(8,128)(2,1)S(1)}, bf16[384,1,1440]{0,2,1:T(8,128)(2,1)S(1)}, bf16[384,1,1440]{0,2,1:T(8,128)(2,1)S(1)}, bf16[384,1,1440]{0,2,1:T(8,128)(2,1)S(1)}) fusion(f32[384]{0:T(512)S(1)} %select_multiply_fusion, s32[384]{0:T(512)} %param.9), kind=kLoop, calls=%fused_computation.36 | loop fusion | flops 9953280 | bytes 4426752 | tf_op jit(solution)/shard_map/convert.2
  13.1 2.5 pad_maximum_fusion
  15.6 6.8 %copy.58 = bf16[384,2,1440]{2,1,0:T(2,128)(2,1)} copy(bf16[384,2,1440]{0,2,1:T(8,128)(2,1)} %get-tuple-element.20) | data formatting | bytes 4423680 | tf_op jit(solution)/shard_map/stack | solution.py:39
  22.4 6.0 %convert_element_type.92 = bf16[768,1440]{1,0:T(8,128)(2,1)} reshape(bf16[384,2,1440]{2,1,0:T(2,128)(2,1)} %copy.58) | data formatting | bytes 4423680 | tf_op jit(solution)/shard_map/convert_element_type | solution.py:39
  28.4 0.0 copy-done.3
  28.4 0.1 select_reduce_fusion.1
  28.5 0.1 dynamic-slice_convert_fusion
  28.6 4.8 %fusion.2 = (f32[256]{0:T(256)S(1)}, f32[256]{0:T(256)S(1)}) fusion(bf16[7,1440,256]{2,1,0:T(8,128)(2,1)} %param.7, f32[7]{0:T(128)S(1)} %dynamic-slice_convert_fusion), kind=kLoop, calls=%fused_computation.8 | loop fusion | flops 12901888 | bytes 5163036 | tf_op jit(solution)/shard_map/reduce_sum | solution.py:65
  33.4 21.9 %all-reduce = (f32[256]{0:T(256)S(1)}, f32[256]{0:T(256)S(1)}) all-reduce(f32[256]{0:T(256)S(1)} %get-tuple-element.6, f32[256]{0:T(256)S(1)} %get-tuple-element.5), channel_id=1, replica_groups=mesh['group'=2,'lat'=16] {'lat'}, use_global_device_ids=true, to_apply=%region_8.9 | all-reduce | flops 512 | bytes 4096 | tf_op jit(solution)/shard_map/psum | solution.py:64
  55.4 9.3 %convert_bitcast_fusion.1 = bf16[7,768,256]{2,1,0:T(8,128)(2,1)} fusion(bf16[7,1440,256]{2,1,0:T(8,128)(2,1)} %param.7, f32[256]{0:T(256)S(1)} %get-tuple-element.16, f32[256]{0:T(256)S(1)} %get-tuple-element.15, f32[7]{0:T(128)S(1)} %dynamic-slice_convert_fusion, bf16[768,1440]{1,0:T(8,128)(2,1)} %convert_element_type.92), kind=kOutput, calls=%fused_computation.23 | convolution fusion | flops 3977895936 | bytes 10127388 | tf_op jit(solution)/shard_map/skc,qk->sqc/dot_general | solution.py:74
  64.6 6.5 %reshape.389 = bf16[7,384,2,256]{3,2,1,0:T(2,128)(2,1)} reshape(bf16[7,768,256]{2,1,0:T(8,128)(2,1)} %convert_bitcast_fusion.1) | data formatting | bytes 5505024 | tf_op jit(solution)/shard_map/reshape | solution.py:75
  71.1 5.2 %copy.60 = bf16[7,384,2,256]{3,2,0,1:T(2,128)(2,1)} copy(bf16[7,384,2,256]{3,2,1,0:T(2,128)(2,1)} %reshape.389) | data formatting | bytes 5505024 | tf_op jit(solution)/shard_map/reshape | solution.py:75
  76.3 16.8 %all-to-all-start = ((bf16[7,384,2,256]{3,2,0,1:T(2,128)(2,1)}), bf16[7,384,2,256]{3,2,0,1:T(2,128)(2,1)}, u32[]{:S(2)}, u32[]{:S(2)}) async-start(bf16[7,384,2,256]{3,2,0,1:T(2,128)(2,1)} %copy.60), calls=%async_computation | async-start | bytes 5505024 | tf_op jit(solution)/shard_map/all_to_all | solution.py:76
  93.1 0.8 dynamic_slice.7
  93.9 0.0 copy-done.1
  93.9 0.2 copy.64
  94.0 0.1 convert_reduce_fusion
  94.1 0.1 select_reduce_fusion
  94.3 0.1 fusion.31
  94.4 60.3 %all-to-all-done = bf16[7,384,2,256]{3,2,0,1:T(2,128)(2,1)} async-done(((bf16[7,384,2,256]{3,2,0,1:T(2,128)(2,1)}), bf16[7,384,2,256]{3,2,0,1:T(2,128)(2,1)}, u32[]{:S(2)}, u32[]{:S(2)}) %all-to-all-start) | async-done | bytes 2752544 | tf_op jit(solution)/shard_map/all_to_all | solution.py:76
  154.7 2.2 copy.61
  156.9 1.8 copy.62
  158.6 4.0 %gather_fusion = bf16[96,24,2,256]{3,1,2,0:T(8,128)(2,1)} fusion(bf16[112,24,2,256]{3,1,2,0:T(8,128)(2,1)} %bitcast.59, s32[1024]{0:T(1024)S(1)} %pad_clamp_fusion.1), kind=kCustom, calls=%fused_computation | custom fusion | bytes 4718976 | tf_op jit(solution)/shard_map/jit(_take)/gather | solution.py:81
  162.7 0.0 copy-done.4
  162.7 2.3 multiply_convert_fusion
  165.0 0.0 copy-done
  165.0 6.1 %fusion = bf16[24,384,2,256]{1,3,2,0:T(8,128)(2,1)} fusion(f32[384,256]{0,1:T(8,128)S(1)} %copy.64, f32[24,384]{1,0:T(8,128)S(1)} %fusion.31, bf16[96,24,2,256]{3,1,2,0:T(8,128)(2,1)S(1)} %multiply_convert_fusion, bf16[24,96,384]{2,1,0:T(8,128)(2,1)S(1)} %copy-done), kind=kOutput, calls=%fused_computation.4 | convolution fusion | flops 920125440 | bytes 13996032 | tf_op jit(solution)/shard_map/rgl,grtc->rltc/dot_general | solution.py:85
  171.1 23.6 %copy.65 = bf16[24,384,2,256]{3,2,1,0:T(2,128)(2,1)} copy(bf16[24,384,2,256]{1,3,2,0:T(8,128)(2,1)} %fusion) | data formatting | bytes 18874368 | tf_op jit(solution)/shard_map/convert_element_type | solution.py:90
  194.7 14.6 %reshape.390 = bf16[18432,256]{1,0:T(8,128)(2,1)} reshape(bf16[24,384,2,256]{3,2,1,0:T(2,128)(2,1)} %copy.65) | data formatting | bytes 18874368 | tf_op jit(solution)/shard_map/reshape | solution.py:91
  209.3 0.0 copy-done.2
  209.3 9.9 %convolution_convert_fusion = bf16[18432,256]{1,0:T(8,128)(2,1)} fusion(bf16[18432,256]{1,0:T(8,128)(2,1)} %reshape.390, bf16[256,256]{1,0:T(8,128)(2,1)S(1)} %copy-done.2), kind=kOutput, calls=%fused_computation.2 | convolution fusion | flops 2420637696 | bytes 19005440 | tf_op jit(solution)/shard_map/dot_general | solution.py:91
  219.2 14.6 %reshape.391 = bf16[24,384,2,256]{3,2,1,0:T(2,128)(2,1)} reshape(bf16[18432,256]{1,0:T(8,128)(2,1)} %convolution_convert_fusion) | data formatting | bytes 18874368 | tf_op jit(solution)/shard_map/reshape | solution.py:92
  233.8 5.6 %convert_bitcast_fusion.2 = bf16[96,24,2,256]{3,0,2,1:T(8,128)(2,1)S(1)} fusion(bf16[24,384,2,256]{3,2,1,0:T(2,128)(2,1)} %reshape.391, bf16[24,96,384]{2,1,0:T(8,128)(2,1)S(1)} %copy-done), kind=kOutput, calls=%fused_computation.27 | convolution fusion | flops 907149312 | bytes 13565952 | tf_op jit(solution)/shard_map/rgl,rltc->grtc/dot_general | solution.py:93
  239.4 2.7 copy.67
  242.2 4.0 %gather_fusion.1 = bf16[112,24,2,256]{3,1,2,0:T(8,128)(2,1)} fusion(bf16[96,24,2,256]{3,1,2,0:T(8,128)(2,1)} %copy.67, s32[1024]{0:T(1024)S(1)} %pad_clamp_fusion), kind=kCustom, calls=%fused_computation.1 | custom fusion | bytes 5505472 | tf_op jit(solution)/shard_map/jit(_take)/gather | solution.py:98
  246.2 3.2 select_select_fusion
  249.4 4.8 %all-to-all-start.1 = ((bf16[112,24,2,256]{3,1,2,0:T(8,128)(2,1)}), bf16[112,24,2,256]{3,1,2,0:T(8,128)(2,1)}, u32[]{:S(2)}, u32[]{:S(2)}) async-start(bf16[112,24,2,256]{3,1,2,0:T(8,128)(2,1)} %select_select_fusion), calls=%async_computation.1 | async-start | bytes 5505024 | tf_op jit(solution)/shard_map/all_to_all | solution.py:102
  254.2 6.9 %copy.56 = bf16[384,2,1440]{2,1,0:T(2,128)(2,1)} copy(bf16[384,2,1440]{0,2,1:T(8,128)(2,1)} %get-tuple-element.19) | data formatting | bytes 4423680 | tf_op jit(solution)/shard_map/stack | solution.py:48
  261.1 6.0 %convert_element_type.90 = bf16[768,1440]{1,0:T(8,128)(2,1)} reshape(bf16[384,2,1440]{2,1,0:T(2,128)(2,1)} %copy.56) | data formatting | bytes 4423680 | tf_op jit(solution)/shard_map/convert_element_type | solution.py:48
  267.1 48.7 %all-to-all-done.1 = bf16[112,24,2,256]{3,1,2,0:T(8,128)(2,1)} async-done(((bf16[112,24,2,256]{3,1,2,0:T(8,128)(2,1)}), bf16[112,24,2,256]{3,1,2,0:T(8,128)(2,1)}, u32[]{:S(2)}, u32[]{:S(2)}) %all-to-all-start.1) | async-done | bytes 2752544 | tf_op jit(solution)/shard_map/all_to_all | solution.py:102
  315.7 5.8 %copy.68 = bf16[7,16,24,2,256]{4,3,2,1,0:T(2,128)(2,1)} copy(bf16[7,16,24,2,256]{4,2,3,0,1:T(8,128)(2,1)} %bitcast.18) | data formatting | bytes 5505024 | tf_op jit(solution)/shard_map/all_to_all | solution.py:102
  321.5 6.8 %reshape.392 = bf16[7,768,256]{2,1,0:T(8,128)(2,1)} reshape(bf16[7,16,24,2,256]{4,3,2,1,0:T(2,128)(2,1)} %copy.68) | data formatting | bytes 5505024 | tf_op jit(solution)/shard_map/reshape | solution.py:103
  328.3 9.1 %convert_bitcast_fusion = bf16[7,1440,256]{2,1,0:T(8,128)(2,1)} fusion(bf16[7,768,256]{2,1,0:T(8,128)(2,1)} %reshape.392, bf16[768,1440]{1,0:T(8,128)(2,1)} %convert_element_type.90), kind=kOutput, calls=%fused_computation.16 | convolution fusion | flops 3966197760 | bytes 10125312 | tf_op jit(solution)/shard_map/sqc,qk->skc/dot_general | solution.py:104
  (14 shorter events, 0.2 us)
Async XLA Ops:
  0.0 165.0 %copy-start = (bf16[24,96,384]{2,1,0:T(8,128)(2,1)S(1)}, bf16[24,96,384]{2,1,0:T(8,128)(2,1)}, u32[]{:S(2)}) copy-start(bf16[24,96,384]{2,1,0:T(8,128)(2,1)} %param.10) | copy-start | bytes 5308420
  22.4 6.0 %copy-start.3 = (s32[16]{0:T(128)S(1)}, s32[16]{0:T(128)}, u32[]{:S(2)}) copy-start(s32[16]{0:T(128)} %param.8) | copy-start | bytes 196
  76.3 17.5 %copy-start.1 = (f32[384,256]{1,0:T(8,128)S(1)}, f32[384,256]{1,0:T(8,128)}, u32[]{:S(2)}) copy-start(f32[384,256]{1,0:T(8,128)} %param.12) | copy-start | bytes 1179652
  76.3 78.3 %all-to-all-start = ((bf16[7,384,2,256]{3,2,0,1:T(2,128)(2,1)}), bf16[7,384,2,256]{3,2,0,1:T(2,128)(2,1)}, u32[]{:S(2)}, u32[]{:S(2)}) async-start(bf16[7,384,2,256]{3,2,0,1:T(2,128)(2,1)} %copy.60), calls=%async_computation | async-start | bytes 5505024 | tf_op jit(solution)/shard_map/all_to_all | solution.py:76
  158.6 4.0 %copy-start.4 = (f32[96]{0:T(128)S(1)}, f32[96]{0:T(128)}, u32[]{:S(2)}) copy-start(f32[96]{0:T(128)} %param.11) | copy-start | bytes 1156
  194.7 14.6 %copy-start.2 = (bf16[256,256]{1,0:T(8,128)(2,1)S(1)}, bf16[256,256]{1,0:T(8,128)(2,1)}, u32[]{:S(2)}) copy-start(bf16[256,256]{1,0:T(8,128)(2,1)} %param.13) | copy-start | bytes 393220
  249.4 66.3 %all-to-all-start.1 = ((bf16[112,24,2,256]{3,1,2,0:T(8,128)(2,1)}), bf16[112,24,2,256]{3,1,2,0:T(8,128)(2,1)}, u32[]{:S(2)}, u32[]{:S(2)}) async-start(bf16[112,24,2,256]{3,1,2,0:T(8,128)(2,1)} %select_select_fusion), calls=%async_computation.1 | async-start | bytes 5505024 | tf_op jit(solution)/shard_map/all_to_all | solution.py:102
where the time goes:
time: 340 us; the launch traced here: 337 us
  local copies, waits for them, and re-layouts  119 us (35%)
  waiting for transfers between devices  109 us (32%)
  matrix products  39.9 us (12%)
  other arithmetic  25.5 us (8%)
  blocking collectives  21.9 us (6%)
  starting transfers between devices  21.5 us (6%)
    all_to_all x1, waiting for transfers between devices, body(): lax.all_to_all(spectra, 'lat', split_axis=1, concat_axis=0, tiled=True)  60.3 us
    all_to_all x1, waiting for transfers between devices, body(): lax.all_to_all(outgoing, 'lat', split_axis=0, concat_axis=1, tiled=True)  48.7 us
    convert_element_type x1, local copies, waits for them, and re-layouts, body(): filtered = (coefficient * degree_mask[:, :, None, None] * spectral_gain[N...  23.6 us
    psum x1, blocking collectives, body(): lax.psum((jnp.sum(widened, axis=(0, 1)), jnp.sum(widened * widened, axis=...  21.9 us
    all_to_all x1, starting transfers between devices, body(): lax.all_to_all(spectra, 'lat', split_axis=1, concat_axis=0, tiled=True)  16.8 us
    reshape x1, local copies, waits for them, and re-layouts, body(): filtered.reshape(-1, channels)  14.6 us
    reshape x1, local copies, waits for them, and re-layouts, body(): mixed = mixed.astype(jnp.bfloat16).reshape(wave_share, degrees, 2, channels)  14.6 us
    reshape x2, local copies, waits for them, and re-layouts, body(): spectra.astype(jnp.bfloat16)  11.7 us
  transfers between devices with their start and end apart: 2, of which 2 were waited for; matrix products, arithmetic and copies ran while one was open for 4% of the time, Pallas kernels for 0%

commit v1 on v0

v1 whole, which is shorter than its diff:
```python
import functools
import math

import jax
import jax.numpy as jnp
from jax import lax
from jax.experimental import pallas as pl
from jax.experimental.pallas import tpu as pltpu
from jax.sharding import PartitionSpec as P

F32 = jnp.float32
BF16 = jnp.bfloat16
LANES = 128
PIECES = 6


def split_waves(share):
    first = share // 2
    return (first, share - first)


def slot_maps(lat_counts, slot_count, live_total):
    devices = lat_counts.shape[0]
    ids = jnp.arange(devices, dtype=jnp.int32)
    starts = jnp.sum(jnp.where(ids[None, :] < ids[:, None], lat_counts[None, :], 0), axis=1)
    within = jnp.arange(slot_count, dtype=jnp.int32)
    valid = within[None, :] < lat_counts[:, None]
    live = starts[:, None] + within[None, :]
    lat = jnp.arange(live_total, dtype=jnp.int32)
    hot = valid[:, :, None] & (live[:, :, None] == lat[None, None, :])
    return hot.reshape(devices * slot_count, live_total)


def angle_of(waves, points, longitudes):
    phase = waves * points % longitudes
    return phase.astype(F32) * (2.0 * math.pi / longitudes)


def row_waves(owner_wavenumber, devices, offset, size):
    share = owner_wavenumber.shape[0] // devices
    part = owner_wavenumber.reshape(devices, share)[:, offset : offset + size]
    waves = jnp.broadcast_to(part[:, None, :], (devices, 2, size)).reshape(-1)
    sine = jnp.broadcast_to(
        jnp.arange(2, dtype=jnp.int32)[None, :, None] == 1, (devices, 2, size)
    ).reshape(-1)
    return waves, sine


def forward_parts(waves, sine, longitudes):
    factor = 1.0 / math.sqrt(longitudes)
    tiles = -(-longitudes // LANES)
    low = sine & (waves == 0)
    head = angle_of(waves[:, None], LANES * jnp.arange(tiles, dtype=jnp.int32)[None, :], longitudes)
    step = angle_of(waves[:, None], jnp.arange(LANES, dtype=jnp.int32)[None, :], longitudes)
    use_sine = (sine & (waves != 0))[:, None]
    cos_head, sin_head = jnp.cos(head) * factor, jnp.sin(head) * factor
    head_a = jnp.where(use_sine, -sin_head, cos_head)
    head_b = jnp.where(use_sine, -cos_head, -sin_head)
    return head_a, head_b, jnp.cos(step), jnp.sin(step), low.astype(F32)[:, None]


def inverse_rows(waves, sine, longitudes):
    factor = 1.0 / math.sqrt(longitudes)
    block = next(b for b in (96, 80, 64, 48, 32, 16, 8, 1) if longitudes % b == 0)
    count = longitudes // block
    head = angle_of(waves[None, :], block * jnp.arange(count, dtype=jnp.int32)[:, None], longitudes)
    step = angle_of(waves[None, :], jnp.arange(block, dtype=jnp.int32)[:, None], longitudes)
    cos_head, sin_head = jnp.cos(head) * factor, jnp.sin(head) * factor
    head_a = jnp.where(sine[None, :], -sin_head, cos_head)
    head_b = jnp.where(sine[None, :], -cos_head, -sin_head)
    table = (
        head_a[:, None, :] * jnp.cos(step)[None] + head_b[:, None, :] * jnp.sin(step)[None]
    ).astype(BF16)
    return table.reshape(longitudes, waves.shape[0])


def dft_kernel(
    count_ref, x_ref, head_a, head_b, step_c, step_s, low_ref, out_ref, sum_ref,
    table, stats, *, slots, devices, rows, with_stats,
):
    slot = pl.program_id(0)
    longitudes = x_ref.shape[0]

    @pl.when(slot == 0)
    def _():
        total = jnp.zeros((devices * rows, 1), F32)
        for i in range(head_a.shape[1]):
            width = min(LANES, longitudes - LANES * i)
            piece = (
                head_a[:, i : i + 1] * step_c[:, :width] + head_b[:, i : i + 1] * step_s[:, :width]
            ).astype(BF16)
            table[:, LANES * i : LANES * i + width] = piece
            total += jnp.sum(piece.astype(F32), axis=1, keepdims=True)
        sum_ref[...] = jnp.broadcast_to(total, sum_ref.shape)
        stats[...] = jnp.zeros_like(stats)

    @pl.when(slot < slots)
    def _():
        acc = jnp.dot(table[...], x_ref[...], preferred_element_type=F32)
        acc = acc - low_ref[...] * acc.astype(BF16).astype(F32)
        for d in range(devices):
            out_ref[d] = acc[d * rows : (d + 1) * rows].astype(BF16)

    if with_stats:

        @pl.when(slot < jnp.minimum(count_ref[0], slots))
        def _():
            x = x_ref[...].astype(F32).reshape(longitudes // 8, 8, x_ref.shape[1])
            stats[0] += jnp.sum(x, axis=0)
            stats[1] += jnp.sum(x * x, axis=0)

        @pl.when(slot == slots)
        def _():
            index = lax.broadcasted_iota(jnp.int32, (rows, x_ref.shape[1]), 0)
            block = jnp.zeros((rows, x_ref.shape[1]), F32)
            for k in range(2):
                rest = jnp.sum(stats[k], axis=0, keepdims=True)
                for piece in range(PIECES // 2):
                    part = rest.astype(BF16).astype(F32)
                    block = jnp.where(index == k * (PIECES // 2) + piece, part, block)
                    rest = rest - part
            block = block.astype(BF16)
            for d in range(devices):
                out_ref[d] = block


def dft(grid_values, count, parts, devices, rows, with_stats):
    slots, longitudes, channels = grid_values.shape
    total = devices * rows
    steps = slots + 1 if with_stats else slots
    if with_stats and rows % 8 == 0:
        out_shape = (devices, slots * rows + 8, channels)
        out_spec = pl.BlockSpec((devices, rows, channels), lambda s: (0, s, 0))
    else:
        out_shape = (devices, steps, rows, channels)
        out_spec = pl.BlockSpec((devices, None, rows, channels), lambda s: (0, s, 0, 0))
    whole = lambda a: pl.BlockSpec(a.shape, lambda s: (0,) * a.ndim)
    return pl.pallas_call(
        functools.partial(
            dft_kernel, slots=slots, devices=devices, rows=rows, with_stats=with_stats
        ),
        grid=(steps,),
        in_specs=[
            pl.BlockSpec(memory_space=pltpu.SMEM),
            pl.BlockSpec(
                (None, longitudes, channels), lambda s: (jnp.minimum(s, slots - 1), 0, 0)
            ),
        ]
        + [whole(a) for a in parts],
        out_specs=[out_spec, pl.BlockSpec((total, LANES), lambda s: (0, 0))],
        out_shape=[
            jax.ShapeDtypeStruct(out_shape, BF16),
            jax.ShapeDtypeStruct((total, LANES), F32),
        ],
        scratch_shapes=[
            pltpu.VMEM((total, longitudes), BF16),
            pltpu.VMEM((2, 8, channels), F32),
        ],
        name="dft_stats" if with_stats else "dft",
    )(count, grid_values, *parts)


def mix_kernel(
    wave_ref, sums_ref, raw_ref, leg_ref, hot_ref, weight_ref, moment_ref, gain_ref, mixer_ref,
    out_ref, *, size,
):
    r = pl.program_id(0)
    wave = wave_ref[r]
    leg = jnp.dot(hot_ref[...], leg_ref[...], preferred_element_type=F32).astype(BF16)
    mean, scale = moment_ref[0:1], moment_ref[1:2]
    gain_row = scale * weight_ref[...]
    zero = (wave == 0).astype(F32)
    low = raw_ref[1].astype(F32)
    first = raw_ref[0].astype(F32) + zero * low
    second = low * (1.0 - zero)
    first = (first - mean * sums_ref[r]) * gain_row
    second = (second - mean * (sums_ref[size + r] * (1.0 - zero))) * gain_row
    weighted = jnp.concatenate([first.astype(BF16), second.astype(BF16)], axis=1)
    coefficient = lax.dot_general(
        leg, weighted, (((0,), (0,)), ((), ())), preferred_element_type=F32
    )
    degrees, channels = gain_ref.shape
    degree = lax.broadcasted_iota(jnp.int32, (degrees, channels), 0)
    gain = jnp.where(degree >= wave, gain_ref[...] * (2.0 - zero), 0.0)
    filtered = jnp.concatenate(
        [
            (coefficient[:, :channels] * gain).astype(BF16),
            (coefficient[:, channels:] * gain).astype(BF16),
        ],
        axis=0,
    )
    mixed = jnp.dot(filtered, mixer_ref[...], preferred_element_type=F32).astype(BF16)
    both = jnp.concatenate([mixed[:degrees], mixed[degrees:]], axis=1)
    synthesis = jnp.dot(leg, both, preferred_element_type=F32).astype(BF16)
    out_ref[0] = synthesis[:, :channels]
    out_ref[1] = synthesis[:, channels:]


def mix(raw, waves, sums, legendre, offset, hot, weight, moments, gain, mixer):
    _, size, slots_all, channels = raw.shape
    _, lats, degrees = legendre.shape
    whole = lambda a: pl.BlockSpec(a.shape, lambda r: (0,) * a.ndim)
    smem = pl.BlockSpec(memory_space=pltpu.SMEM)
    block = pl.BlockSpec((2, None, slots_all, channels), lambda r: (0, r, 0, 0))
    return pl.pallas_call(
        functools.partial(mix_kernel, size=size),
        grid=(size,),
        in_specs=[
            smem,
            smem,
            block,
            pl.BlockSpec((None, lats, degrees), lambda r: (r + offset, 0, 0)),
            whole(hot),
            whole(weight),
            whole(moments),
            whole(gain),
            whole(mixer),
        ],
        out_specs=block,
        out_shape=jax.ShapeDtypeStruct(raw.shape, BF16),
        name="mix",
    )(waves, sums, raw, legendre, hot, weight, moments, gain, mixer)


def final_kernel(table_ref, *refs):
    *parts, out_ref, gathered = refs
    at = 0
    for part in parts:
        devices, rows, _ = part.shape
        for d in range(devices):
            gathered[at : at + rows] = part[d]
            at += rows
    out_ref[...] = jnp.dot(
        table_ref[...], gathered[...], preferred_element_type=F32
    ).astype(BF16)


def final(table, parts):
    longitudes, total = table.shape
    devices, slots, _, channels = parts[0].shape
    return pl.pallas_call(
        final_kernel,
        grid=(slots,),
        in_specs=[pl.BlockSpec(table.shape, lambda s: (0, 0))]
        + [
            pl.BlockSpec((devices, None, p.shape[2], channels), lambda s: (0, s, 0, 0))
            for p in parts
        ],
        out_specs=pl.BlockSpec((None, longitudes, channels), lambda s: (s, 0, 0)),
        out_shape=jax.ShapeDtypeStruct((slots, longitudes, channels), BF16),
        scratch_shapes=[pltpu.VMEM((total, channels), BF16)],
        name="inverse",
    )(table, *parts)


def body(
    grid_values, lat_counts, owner_wavenumber, legendre, quad_weight, spectral_gain, channel_mix
):
    slots, longitudes, channels = grid_values.shape
    devices = lat_counts.shape[0]
    share, live_total, _ = legendre.shape
    me = lax.axis_index("lat")
    exchange = lambda a: lax.all_to_all(a, "lat", split_axis=0, concat_axis=0, tiled=True)
    count = lax.dynamic_slice_in_dim(lat_counts, me, 1)
    sizes = split_waves(share)
    offsets = [sum(sizes[:h]) for h in range(len(sizes))]
    rows_of = [
        row_waves(owner_wavenumber, devices, o, n) for o, n in zip(offsets, sizes)
    ]

    received, own_sums = [], []
    for h, size in enumerate(sizes):
        out, sums = dft(
            grid_values, count, forward_parts(*rows_of[h], longitudes), devices, 2 * size, h == 0
        )
        own_sums.append(lax.dynamic_slice(sums, (me * 2 * size, 0), (2 * size, 1))[:, 0])
        received.append(exchange(out))

    hot = slot_maps(lat_counts, slots, live_total)
    weight = jnp.sum(jnp.where(hot, quad_weight[None, :], 0.0), axis=1)[:, None]
    hot = hot.astype(BF16)
    flat = received[0].reshape(devices, -1, channels)
    body_rows = slots * 2 * sizes[0]
    pieces = jnp.sum(
        flat[:, body_rows : body_rows + PIECES].astype(F32).reshape(devices, 2, PIECES // 2, channels),
        axis=2,
    )
    totals = jnp.sum(pieces, axis=0) / (live_total * longitudes)
    variance = totals[1] - totals[0] * totals[0]
    moments = jnp.stack([totals[0], lax.rsqrt(variance + 1e-05)])
    received[0] = flat[:, :body_rows]

    returned = []
    for h, size in enumerate(sizes):
        raw = received[h].reshape(devices * slots, 2, size, channels).transpose(1, 2, 0, 3)
        waves = lax.dynamic_slice_in_dim(owner_wavenumber, me * share + offsets[h], size)
        synthesis = mix(
            raw, waves, own_sums[h], legendre, offsets[h], hot, weight, moments,
            spectral_gain, channel_mix,
        )
        outgoing = synthesis.reshape(2 * size, devices, slots, channels).transpose(1, 2, 0, 3)
        returned.append(exchange(outgoing))

    waves = jnp.concatenate([w for w, _ in rows_of])
    sine = jnp.concatenate([s for _, s in rows_of])
    return final(inverse_rows(waves, sine, longitudes), returned)


def solution(mesh):
    return jax.shard_map(
        body,
        mesh=mesh,
        in_specs=(P(("group", "lat"), None, None), P(), P(), P("lat", None, None), P(), P(), P()),
        out_specs=P(("group", "lat"), None, None),
        check_vma=False,
    )
```

time: 340 us -> 200 us (0.59)
  local copies, waits for them, and re-layouts: 119 us -> 25.7 us
  Pallas kernels: 0 us -> 56.8 us
  matrix products: 39.9 us -> 0 us
  waiting for transfers between devices: 109 us -> 83.1 us
  blocking collectives: 21.9 us -> 0 us
  other arithmetic: 25.5 us -> 11.7 us
    pallas_call x0 -> x5, Pallas kernels: none -> 56.8 us  [the longest x2 25.2 us: mix(): pl.pallas_call(functools.partial(mix_kernel, size=size), grid=(size,), in...]
    dot_general x5 -> x0, matrix products: 39.9 us -> none  [the longest x1 9.92 us: body(): jnp.dot(filtered.reshape(-1, channels), channel_mix, preferred_element_ty...]
    convert_element_type x4 -> x2, local copies, waits for them, and re-layouts: 38.4 us -> 1.61 us  [forward_parts(): low.astype(F32)[:, None]]
    reshape x5 -> x12, local copies, waits for them, and re-layouts: 47.7 us -> 16.1 us  [the longest x4 8.59 us: body(): synthesis.reshape(2 * size, devices, slots, channels).transpose(1, 2, 0, 3)]
    all_to_all x2 -> x4, waiting for transfers between devices: 109 us -> 83.1 us  [body(): lax.all_to_all(a, 'lat', split_axis=0, concat_axis=0, tiled=True)]
    psum x1 -> x0, blocking collectives: 21.9 us -> none  [body(): lax.psum((jnp.sum(widened, axis=(0, 1)), jnp.sum(widened * widened, axis=...]
    another operation x3 -> x0, local copies, waits for them, and re-layouts: 14.5 us -> none  [the longest x1 6.89 us: inverse_table(): jnp.stack([jnp.cos(angle) * doubled, -jnp.sin(angle) * doubled], axis=1)]
    another operation x4 -> x1, other arithmetic: 13.4 us -> 0.59 us  [body(): moments = jnp.stack([totals[0], lax.rsqrt(variance + 1e-05)])]
  transfers between devices with their start and end apart: 2 -> 4, of which waited for: 2 -> 4; matrix products, arithmetic and copies ran while one was open for 4% -> 11% of each run, Pallas kernels for 0% -> 12%
where the time goes in v1:
time: 200 us; the launch traced here: 198 us
  waiting for transfers between devices  83.1 us (42%)
  Pallas kernels  56.8 us (28%)
  local copies, waits for them, and re-layouts  25.7 us (13%)
  starting transfers between devices  20.7 us (10%)
  other arithmetic  11.7 us (6%)
    all_to_all x4, waiting for transfers between devices, body(): lax.all_to_all(a, 'lat', split_axis=0, concat_axis=0, tiled=True)  83.1 us
    pallas_call x2, Pallas kernels, mix(): pl.pallas_call(functools.partial(mix_kernel, size=size), grid=(size,), in...  25.2 us
    pallas_call x2, Pallas kernels, dft(): pl.pallas_call(functools.partial(dft_kernel, slots=slots, devices=devices...  21.9 us
    all_to_all x4, starting transfers between devices, body(): lax.all_to_all(a, 'lat', split_axis=0, concat_axis=0, tiled=True)  20.7 us
    pallas_call x1, Pallas kernels, final(): pl.pallas_call(final_kernel, grid=(slots,), in_specs=[pl.BlockSpec(table....  9.65 us
    reshape x4, local copies, waits for them, and re-layouts, body(): synthesis.reshape(2 * size, devices, slots, channels).transpose(1, 2, 0, 3)  8.59 us
    reshape x4, local copies, waits for them, and re-layouts, body(): received[h].reshape(devices * slots, 2, size, channels)  6.37 us
  transfers between devices with their start and end apart: 4, of which 4 were waited for; matrix products, arithmetic and copies ran while one was open for 11% of the time, Pallas kernels for 12%

profile of v1, /device:TPU:15, one launch (start us, length us, event | category | flops | bytes accessed | tf_op | source)
XLA Modules:
  0.0 198.3 jit_solution(15466072478503387978)
XLA Ops:
  0.0 0.8 reshape.309
  1.0 0.1 reshape.308
  1.1 0.1 reshape.311
  1.3 0.1 reshape.310
  1.4 0.1 and_convert_fusion
  1.5 0.8 reshape.319.low_ref
  2.3 1.7 fusion.17
  3.9 1.2 dynamic_slice.16.count_ref
  5.2 2.9 %negate_select_fusion = (f32[384,12]{1,0:T(8,128)}, f32[384,12]{1,0:T(8,128)}, f32[384,12]{1,0:T(8,128)}, f32[384,12]{1,0:T(8,128)}) fusion(s32[384]{0:T(512)S(1)} %reshape.311, s32[12]{0:T(128)S(1)} %iota_multiply_fusion, pred[384]{0:T(512)(128)(4,1)S(1)} %get-tuple-element.37, s32[384]{0:T(512)S(1)} %reshape.310, pred[384]{0:T(512)(128)(4,1)S(1)} %get-tuple-element.38), kind=kLoop, calls=%fused_computation.31 | loop fusion | flops 138240 | bytes 77616 | tf_op jit(solution)/shard_map/jit(_where)/select_n | solution.py:58
  8.1 10.6 %dft.1 = (bf16[16,7,24,256]{3,2,1,0:T(8,128)(2,1)}, f32[384,128]{1,0:T(8,128)}) custom-call(s32[1]{0:T(128)} %dynamic_slice.16.count_ref, bf16[7,1440,256]{2,1,0:T(8,128)(2,1)} %x_ref.3, f32[384,12]{1,0:T(8,128)} %get-tuple-element.22.head_a, f32[384,12]{1,0:T(8,128)} %get-tuple-element.21.head_b, f32[384,128]{1,0:T(8,128)} %get-tuple-element.26.step_c, ...), custom_call_target="tpu_custom_call" | custom-call | tf_op jit(solution)/shard_map/dft/pallas_call | solution.py:138
  18.7 6.5 %all-to-all-start.2 = ((bf16[16,7,24,256]{3,2,1,0:T(8,128)(2,1)}), bf16[16,7,24,256]{3,2,1,0:T(8,128)(2,1)S(1)}, u32[]{:S(2)}, u32[]{:S(2)}) async-start(bf16[16,7,24,256]{3,2,1,0:T(8,128)(2,1)} %get-tuple-element.12), calls=%async_computation.2 | async-start | bytes 2752512 | tf_op jit(solution)/shard_map/all_to_all | solution.py:263
  25.2 0.8 reshape.318.low_ref
  26.1 1.7 fusion.23
  27.7 11.3 %dft_stats.1 = (bf16[16,176,256]{2,1,0:T(8,128)(2,1)}, f32[384,128]{1,0:T(8,128)}) custom-call(s32[1]{0:T(128)} %dynamic_slice.16.count_ref, bf16[7,1440,256]{2,1,0:T(8,128)(2,1)} %x_ref.3, f32[384,12]{1,0:T(8,128)} %get-tuple-element.35.head_a, f32[384,12]{1,0:T(8,128)} %get-tuple-element.36.head_b, f32[384,128]{1,0:T(8,128)} %get-tuple-element.32.step_c, ...), custom_call_target="tpu_custom_call" | custom-call | tf_op jit(solution)/shard_map/dft_stats/pallas_call | solution.py:138
  39.1 18.2 %all-to-all-done.2 = bf16[16,7,24,256]{3,2,1,0:T(8,128)(2,1)S(1)} async-done(((bf16[16,7,24,256]{3,2,1,0:T(8,128)(2,1)}), bf16[16,7,24,256]{3,2,1,0:T(8,128)(2,1)S(1)}, u32[]{:S(2)}, u32[]{:S(2)}) %all-to-all-start.2) | async-done | bytes 1376288 | tf_op jit(solution)/shard_map/all_to_all | solution.py:263
  57.2 1.1 copy-done.1
  58.3 4.7 %all-to-all-start = ((bf16[16,176,256]{2,1,0:T(8,128)(2,1)}), bf16[16,176,256]{2,1,0:T(8,128)(2,1)S(1)}, u32[]{:S(2)}, u32[]{:S(2)}) async-start(bf16[16,176,256]{2,1,0:T(8,128)(2,1)} %get-tuple-element.10), calls=%async_computation | async-start | bytes 2883584 | tf_op jit(solution)/shard_map/all_to_all | solution.py:263
  63.1 0.1 lt.87
  63.2 0.1 select_reduce_fusion.1
  63.4 0.1 add.101
  63.5 0.2 select_reduce_fusion
  63.7 0.7 copy.23.weight_ref
  64.5 1.4 dynamic-slice_reduce_fusion.sums_ref
  65.9 0.6 fusion.44
  66.5 0.7 fusion.34.hot_ref
  67.2 2.3 %reshape.320 = bf16[112,2,12,256]{3,2,1,0:T(8,128)(2,1)S(1)} reshape(bf16[16,7,24,256]{3,2,1,0:T(8,128)(2,1)} %copy-done.1) | data formatting | bytes 2752512 | tf_op jit(solution)/shard_map/reshape | solution.py:295
  69.5 1.9 copy.34
  71.4 25.1 %all-to-all-done = bf16[16,176,256]{2,1,0:T(8,128)(2,1)S(1)} async-done(((bf16[16,176,256]{2,1,0:T(8,128)(2,1)}), bf16[16,176,256]{2,1,0:T(8,128)(2,1)S(1)}, u32[]{:S(2)}, u32[]{:S(2)}) %all-to-all-start) | async-done | bytes 1441824 | tf_op jit(solution)/shard_map/all_to_all | solution.py:263
  96.5 0.6 pad_maximum_fusion.moment_ref
  97.1 12.6 %mix.3 = bf16[2,12,112,256]{3,2,1,0:T(8,128)(2,1)} custom-call(s32[12]{0:T(128)} %get-tuple-element.27.wave_ref, f32[24]{0:T(128)} %dynamic-slice_reduce_fusion.sums_ref, bf16[2,12,112,256]{3,2,1,0:T(8,128)(2,1)} %bitcast.22, bf16[24,96,384]{2,1,0:T(8,128)(2,1)} %leg_ref.3, bf16[112,96]{1,0:T(8,128)(2,1)} %fusion.34.hot_ref, f32[112,1]{1,0:T(8,128)} %copy.23.weight_ref, ...), custom_call_target="tpu_custom_call" | custom-call | tf_op jit(solution)/shard_map/mix/pallas_call | solution.py:205
  109.7 2.3 %reshape.315 = bf16[24,16,7,256]{3,2,1,0:T(8,128)(2,1)S(1)} reshape(bf16[2,12,112,256]{3,2,1,0:T(8,128)(2,1)} %mix.3) | data formatting | bytes 2752512 | tf_op jit(solution)/shard_map/reshape | solution.py:301
  112.1 2.0 copy.35
  114.0 4.7 %all-to-all-start.3 = ((bf16[16,7,24,256]{3,2,1,0:T(8,128)(2,1)}), bf16[16,7,24,256]{3,2,1,0:T(8,128)(2,1)}, u32[]{:S(2)}, u32[]{:S(2)}) async-start(bf16[16,7,24,256]{3,2,1,0:T(8,128)(2,1)} %bitcast.21), calls=%async_computation.3 | async-start | bytes 2752512 | tf_op jit(solution)/shard_map/all_to_all | solution.py:263
  118.8 1.4 dynamic-slice_reduce_fusion.1.sums_ref
  120.1 0.1 slice.28
  120.2 0.3 reshape.312
  120.6 1.8 copy.37
  122.4 12.6 %mix.2 = bf16[2,12,112,256]{3,2,1,0:T(8,128)(2,1)} custom-call(s32[12]{0:T(128)} %get-tuple-element.28.wave_ref, f32[24]{0:T(128)} %dynamic-slice_reduce_fusion.1.sums_ref, bf16[2,12,112,256]{3,2,1,0:T(8,128)(2,1)} %bitcast.23, bf16[24,96,384]{2,1,0:T(8,128)(2,1)} %leg_ref.3, bf16[112,96]{1,0:T(8,128)(2,1)} %fusion.34.hot_ref, f32[112,1]{1,0:T(8,128)} %copy.23.weight_ref, ...), custom_call_target="tpu_custom_call" | custom-call | tf_op jit(solution)/shard_map/mix/pallas_call | solution.py:205
  135.0 2.3 %reshape.313 = bf16[24,16,7,256]{3,2,1,0:T(8,128)(2,1)S(1)} reshape(bf16[2,12,112,256]{3,2,1,0:T(8,128)(2,1)} %mix.2) | data formatting | bytes 2752512 | tf_op jit(solution)/shard_map/reshape | solution.py:301
  137.4 1.9 copy.36
  139.3 11.5 %all-to-all-done.3.refs_1_ = bf16[16,7,24,256]{3,2,1,0:T(8,128)(2,1)} async-done(((bf16[16,7,24,256]{3,2,1,0:T(8,128)(2,1)}), bf16[16,7,24,256]{3,2,1,0:T(8,128)(2,1)}, u32[]{:S(2)}, u32[]{:S(2)}) %all-to-all-start.3) | async-done | bytes 1376288 | tf_op jit(solution)/shard_map/all_to_all | solution.py:263
  150.8 4.7 %all-to-all-start.1 = ((bf16[16,7,24,256]{3,2,1,0:T(8,128)(2,1)}), bf16[16,7,24,256]{3,2,1,0:T(8,128)(2,1)S(1)}, u32[]{:S(2)}, u32[]{:S(2)}) async-start(bf16[16,7,24,256]{3,2,1,0:T(8,128)(2,1)} %bitcast.18), calls=%async_computation.1 | async-start | bytes 2752512 | tf_op jit(solution)/shard_map/all_to_all | solution.py:263
  155.6 0.3 fusion.40
  155.9 1.2 fusion.5
  157.2 2.0 %add_convert_fusion = bf16[15,96,768]{2,1,0:T(8,128)(2,1)} fusion(f32[96,768]{1,0:T(8,128)S(1)} %get-tuple-element.20, f32[15,768]{1,0:T(8,128)S(1)} %get-tuple-element.18, f32[96,768]{1,0:T(8,128)S(1)} %get-tuple-element.19, f32[15,768]{1,0:T(8,128)S(1)} %get-tuple-element.17), kind=kLoop, calls=%fused_computation | loop fusion | flops 4423680 | bytes 2893824 | tf_op jit(solution)/shard_map/convert_element_type | solution.py:73
  159.2 28.4 %all-to-all-done.1.refs_0_ = bf16[16,7,24,256]{3,2,1,0:T(8,128)(2,1)S(1)} async-done(((bf16[16,7,24,256]{3,2,1,0:T(8,128)(2,1)}), bf16[16,7,24,256]{3,2,1,0:T(8,128)(2,1)S(1)}, u32[]{:S(2)}, u32[]{:S(2)}) %all-to-all-start.1) | async-done | bytes 1376288 | tf_op jit(solution)/shard_map/all_to_all | solution.py:263
  187.6 1.1 copy-done
  188.7 9.6 %inverse.1 = bf16[7,1440,256]{2,1,0:T(8,128)(2,1)} custom-call(bf16[1440,768]{1,0:T(8,128)(2,1)} %bitcast.20, bf16[16,7,24,256]{3,2,1,0:T(8,128)(2,1)} %copy-done, bf16[16,7,24,256]{3,2,1,0:T(8,128)(2,1)} %all-to-all-done.3.refs_1_), custom_call_target="tpu_custom_call" | custom-call | tf_op jit(solution)/shard_map/inverse/pallas_call | solution.py:241
  (28 shorter events, 0.5 us)
Async XLA Ops:
  18.7 38.5 %all-to-all-start.2 = ((bf16[16,7,24,256]{3,2,1,0:T(8,128)(2,1)}), bf16[16,7,24,256]{3,2,1,0:T(8,128)(2,1)S(1)}, u32[]{:S(2)}, u32[]{:S(2)}) async-start(bf16[16,7,24,256]{3,2,1,0:T(8,128)(2,1)} %get-tuple-element.12), calls=%async_computation.2 | async-start | bytes 2752512 | tf_op jit(solution)/shard_map/all_to_all | solution.py:263
  39.0 24.0 %copy-start.3 = (s32[16]{0:T(128)S(1)}, s32[16]{0:T(128)}, u32[]{:S(2)}) copy-start(s32[16]{0:T(128)} %param.8) | copy-start | bytes 196
  39.0 24.5 %copy-start.4 = (f32[96]{0:T(128)S(1)}, f32[96]{0:T(128)}, u32[]{:S(2)}) copy-start(f32[96]{0:T(128)} %param.11) | copy-start | bytes 1156
  39.0 26.8 %copy-start.2 = (s32[384]{0:T(512)S(1)}, s32[384]{0:T(512)}, u32[]{:S(2)}) copy-start(s32[384]{0:T(512)} %param.9) | copy-start | bytes 4612
  57.2 1.1 copy-start.1
  58.3 38.1 %all-to-all-start = ((bf16[16,176,256]{2,1,0:T(8,128)(2,1)}), bf16[16,176,256]{2,1,0:T(8,128)(2,1)S(1)}, u32[]{:S(2)}, u32[]{:S(2)}) async-start(bf16[16,176,256]{2,1,0:T(8,128)(2,1)} %get-tuple-element.10), calls=%async_computation | async-start | bytes 2883584 | tf_op jit(solution)/shard_map/all_to_all | solution.py:263
  114.0 36.8 %all-to-all-start.3 = ((bf16[16,7,24,256]{3,2,1,0:T(8,128)(2,1)}), bf16[16,7,24,256]{3,2,1,0:T(8,128)(2,1)}, u32[]{:S(2)}, u32[]{:S(2)}) async-start(bf16[16,7,24,256]{3,2,1,0:T(8,128)(2,1)} %bitcast.21), calls=%async_computation.3 | async-start | bytes 2752512 | tf_op jit(solution)/shard_map/all_to_all | solution.py:263
  150.8 36.7 %all-to-all-start.1 = ((bf16[16,7,24,256]{3,2,1,0:T(8,128)(2,1)}), bf16[16,7,24,256]{3,2,1,0:T(8,128)(2,1)S(1)}, u32[]{:S(2)}, u32[]{:S(2)}) async-start(bf16[16,7,24,256]{3,2,1,0:T(8,128)(2,1)} %bitcast.18), calls=%async_computation.1 | async-start | bytes 2752512 | tf_op jit(solution)/shard_map/all_to_all | solution.py:263
  187.5 1.1 copy-start

commit v2 on v1

--- a/solution.py
+++ b/solution.py
@@ -103,7 +103,7 @@
 
     if with_stats:
 
-        @pl.when(slot < jnp.minimum(count_ref[0], slots))
+        @pl.when(slot < jnp.minimum(count_ref[lax.axis_index("lat")], slots))
         def _():
             x = x_ref[...].astype(F32).reshape(longitudes // 8, 8, x_ref.shape[1])
             stats[0] += jnp.sum(x, axis=0)
@@ -261,7 +261,6 @@
     share, live_total, _ = legendre.shape
     me = lax.axis_index("lat")
     exchange = lambda a: lax.all_to_all(a, "lat", split_axis=0, concat_axis=0, tiled=True)
-    count = lax.dynamic_slice_in_dim(lat_counts, me, 1)
     sizes = split_waves(share)
     offsets = [sum(sizes[:h]) for h in range(len(sizes))]
     rows_of = [
@@ -270,8 +269,12 @@
 
     received, own_sums = [], []
     for h, size in enumerate(sizes):
+        waves, sine = rows_of[h]
+        if h > 0:
+            waves, _ = lax.optimization_barrier((waves, sums))
         out, sums = dft(
-            grid_values, count, forward_parts(*rows_of[h], longitudes), devices, 2 * size, h == 0
+            grid_values, lat_counts, forward_parts(waves, sine, longitudes), devices, 2 * size,
+            h == 0,
         )
         own_sums.append(lax.dynamic_slice(sums, (me * 2 * size, 0), (2 * size, 1))[:, 0])
         received.append(exchange(out))

time: 200 us -> 179 us (0.90)
  waiting for transfers between devices: 83.1 us -> 61.5 us
    all_to_all x4, waiting for transfers between devices: 83.1 us -> 61.5 us  [body(): lax.all_to_all(a, 'lat', split_axis=0, concat_axis=0, tiled=True)]
  transfers between devices with their start and end apart: 4 -> 4, of which waited for: 4 -> 4; matrix products, arithmetic and copies ran while one was open for 11% -> 18% of each run, Pallas kernels for 12% -> 20%
where the time goes in v2:
time: 179 us; the launch traced here: 177 us
  waiting for transfers between devices  61.5 us (34%)
  Pallas kernels  55.8 us (31%)
  local copies, waits for them, and re-layouts  26.5 us (15%)
  starting transfers between devices  20.9 us (12%)
  other arithmetic  12.4 us (7%)
    all_to_all x4, waiting for transfers between devices, body(): lax.all_to_all(a, 'lat', split_axis=0, concat_axis=0, tiled=True)  61.5 us
    pallas_call x2, Pallas kernels, mix(): pl.pallas_call(functools.partial(mix_kernel, size=size), grid=(size,), in...  25.3 us
    all_to_all x4, starting transfers between devices, body(): lax.all_to_all(a, 'lat', split_axis=0, concat_axis=0, tiled=True)  20.9 us
    pallas_call x2, Pallas kernels, dft(): pl.pallas_call(functools.partial(dft_kernel, slots=slots, devices=devices...  20.9 us
    pallas_call x1, Pallas kernels, final(): pl.pallas_call(final_kernel, grid=(slots,), in_specs=[pl.BlockSpec(table....  9.65 us
    reshape x4, local copies, waits for them, and re-layouts, body(): synthesis.reshape(2 * size, devices, slots, channels).transpose(1, 2, 0, 3)  8.59 us
    reshape x4, local copies, waits for them, and re-layouts, body(): received[h].reshape(devices * slots, 2, size, channels)  8.33 us
  transfers between devices with their start and end apart: 4, of which 4 were waited for; matrix products, arithmetic and copies ran while one was open for 18% of the time, Pallas kernels for 20%

profile of v2, /device:TPU:15, one launch (start us, length us, event | category | flops | bytes accessed | tf_op | source)
XLA Modules:
  0.0 177.3 jit_solution(3357575897634055657)
XLA Ops:
  0.0 0.8 reshape.274
  0.9 0.1 broadcast_in_dim.126
  0.9 0.1 reshape.273
  1.1 0.1 and_convert_fusion
  1.2 0.1 reshape.275
  1.3 1.7 fusion.23
  3.0 0.8 reshape.283.low_ref
  3.8 1.8 negate_select_fusion.1
  5.6 10.8 %dft_stats.1 = (bf16[16,176,256]{2,1,0:T(8,128)(2,1)}, f32[384,128]{1,0:T(8,128)}) custom-call(s32[16]{0:T(128)} %count_ref.3, bf16[7,1440,256]{2,1,0:T(8,128)(2,1)} %x_ref.3, f32[384,12]{1,0:T(8,128)} %get-tuple-element.24.head_a, f32[384,12]{1,0:T(8,128)} %get-tuple-element.23.head_b, f32[384,128]{1,0:T(8,128)} %get-tuple-element.34.step_c, ...), custom_call_target="tpu_custom_call" | custom-call | tf_op jit(solution)/shard_map/dft_stats/pallas_call | solution.py:138
  16.4 6.7 %all-to-all-start = ((bf16[16,176,256]{2,1,0:T(8,128)(2,1)}), bf16[16,176,256]{2,1,0:T(8,128)(2,1)S(1)}, u32[]{:S(2)}, u32[]{:S(2)}) async-start(bf16[16,176,256]{2,1,0:T(8,128)(2,1)} %get-tuple-element.11), calls=%async_computation | async-start | bytes 2883584 | tf_op jit(solution)/shard_map/all_to_all | solution.py:263
  23.1 0.1 reshape.276
  23.2 0.8 reshape.284.low_ref
  24.0 1.7 fusion.17
  25.7 1.8 %negate_select_fusion = (f32[384,12]{1,0:T(8,128)}, f32[384,12]{1,0:T(8,128)}) fusion(s32[384]{0:T(512)S(1)} %reshape.276, s32[12]{0:T(128)S(1)} %iota_multiply_fusion, pred[384]{0:T(512)(128)(4,1)S(1)} %get-tuple-element.26), kind=kLoop, calls=%fused_computation.31 | loop fusion | flops 69120 | bytes 38832 | tf_op jit(solution)/shard_map/jit(_where)/select_n | solution.py:58
  27.5 10.1 %dft.1 = (bf16[16,7,24,256]{3,2,1,0:T(8,128)(2,1)}, f32[384,128]{1,0:T(8,128)}) custom-call(s32[16]{0:T(128)} %count_ref.3, bf16[7,1440,256]{2,1,0:T(8,128)(2,1)} %x_ref.3, f32[384,12]{1,0:T(8,128)} %get-tuple-element.22.head_a, f32[384,12]{1,0:T(8,128)} %get-tuple-element.21.head_b, f32[384,128]{1,0:T(8,128)} %get-tuple-element.28.step_c, ...), custom_call_target="tpu_custom_call" | custom-call | tf_op jit(solution)/shard_map/dft/pallas_call | solution.py:138
  37.6 18.8 %all-to-all-done = bf16[16,176,256]{2,1,0:T(8,128)(2,1)S(1)} async-done(((bf16[16,176,256]{2,1,0:T(8,128)(2,1)}), bf16[16,176,256]{2,1,0:T(8,128)(2,1)S(1)}, u32[]{:S(2)}, u32[]{:S(2)}) %all-to-all-start) | async-done | bytes 1441824 | tf_op jit(solution)/shard_map/all_to_all | solution.py:263
  56.4 4.7 %all-to-all-start.2 = ((bf16[16,7,24,256]{3,2,1,0:T(8,128)(2,1)}), bf16[16,7,24,256]{3,2,1,0:T(8,128)(2,1)S(1)}, u32[]{:S(2)}, u32[]{:S(2)}) async-start(bf16[16,7,24,256]{3,2,1,0:T(8,128)(2,1)} %get-tuple-element.14), calls=%async_computation.2 | async-start | bytes 2752512 | tf_op jit(solution)/shard_map/all_to_all | solution.py:263
  61.3 0.1 lt.83
  61.4 0.1 select_reduce_fusion.1
  61.5 0.1 add.97
  61.7 0.2 select_reduce_fusion
  61.8 0.8 copy.23.weight_ref
  62.6 1.4 dynamic-slice_reduce_fusion.1.sums_ref
  64.0 0.7 fusion.44
  64.6 0.7 fusion.34.hot_ref
  65.4 1.2 slice.28
  66.5 2.3 %reshape.277 = bf16[112,2,12,256]{3,2,1,0:T(8,128)(2,1)S(1)} reshape(bf16[16,168,256]{2,1,0:T(8,128)(2,1)} %slice.28) | data formatting | bytes 2752512 | tf_op jit(solution)/shard_map/reshape | solution.py:298
  68.9 1.8 %copy.37 = bf16[112,2,12,256]{3,0,2,1:T(8,128)(2,1)} copy(bf16[112,2,12,256]{3,2,1,0:T(8,128)(2,1)S(1)} %reshape.277) | data formatting | bytes 2752512 | tf_op jit(solution)/shard_map/reshape | solution.py:298
  70.7 0.6 pad_maximum_fusion.moment_ref
  71.4 12.6 %mix.2 = bf16[2,12,112,256]{3,2,1,0:T(8,128)(2,1)} custom-call(s32[12]{0:T(128)} %get-tuple-element.30.wave_ref, f32[24]{0:T(128)} %dynamic-slice_reduce_fusion.1.sums_ref, bf16[2,12,112,256]{3,2,1,0:T(8,128)(2,1)} %bitcast.23, bf16[24,96,384]{2,1,0:T(8,128)(2,1)} %leg_ref.3, bf16[112,96]{1,0:T(8,128)(2,1)} %fusion.34.hot_ref, f32[112,1]{1,0:T(8,128)} %copy.23.weight_ref, ...), custom_call_target="tpu_custom_call" | custom-call | tf_op jit(solution)/shard_map/mix/pallas_call | solution.py:205
  84.0 2.3 %reshape.278 = bf16[24,16,7,256]{3,2,1,0:T(8,128)(2,1)S(1)} reshape(bf16[2,12,112,256]{3,2,1,0:T(8,128)(2,1)} %mix.2) | data formatting | bytes 2752512 | tf_op jit(solution)/shard_map/reshape | solution.py:304
  86.3 1.9 %copy.36 = bf16[24,16,7,256]{3,0,2,1:T(8,128)(2,1)} copy(bf16[24,16,7,256]{3,2,1,0:T(8,128)(2,1)S(1)} %reshape.278) | data formatting | bytes 2752512 | tf_op jit(solution)/shard_map/reshape | solution.py:304
  88.3 4.9 %all-to-all-done.2 = bf16[16,7,24,256]{3,2,1,0:T(8,128)(2,1)S(1)} async-done(((bf16[16,7,24,256]{3,2,1,0:T(8,128)(2,1)}), bf16[16,7,24,256]{3,2,1,0:T(8,128)(2,1)S(1)}, u32[]{:S(2)}, u32[]{:S(2)}) %all-to-all-start.2) | async-done | bytes 1376288 | tf_op jit(solution)/shard_map/all_to_all | solution.py:263
  93.2 4.7 %all-to-all-start.1 = ((bf16[16,7,24,256]{3,2,1,0:T(8,128)(2,1)}), bf16[16,7,24,256]{3,2,1,0:T(8,128)(2,1)S(1)}, u32[]{:S(2)}, u32[]{:S(2)}) async-start(bf16[16,7,24,256]{3,2,1,0:T(8,128)(2,1)} %bitcast.22), calls=%async_computation.1 | async-start | bytes 2752512 | tf_op jit(solution)/shard_map/all_to_all | solution.py:263
  97.9 1.4 dynamic-slice_reduce_fusion.sums_ref
  99.3 2.3 %reshape.285 = bf16[112,2,12,256]{3,2,1,0:T(8,128)(2,1)S(1)} reshape(bf16[16,7,24,256]{3,2,1,0:T(8,128)(2,1)} %copy-done.2) | data formatting | bytes 2752512 | tf_op jit(solution)/shard_map/reshape | solution.py:298
  101.6 1.9 %copy.34 = bf16[112,2,12,256]{3,0,2,1:T(8,128)(2,1)} copy(bf16[112,2,12,256]{3,2,1,0:T(8,128)(2,1)S(1)} %reshape.285) | data formatting | bytes 2752512 | tf_op jit(solution)/shard_map/reshape | solution.py:298
  103.5 12.6 %mix.3 = bf16[2,12,112,256]{3,2,1,0:T(8,128)(2,1)} custom-call(s32[12]{0:T(128)} %get-tuple-element.29.wave_ref, f32[24]{0:T(128)} %dynamic-slice_reduce_fusion.sums_ref, bf16[2,12,112,256]{3,2,1,0:T(8,128)(2,1)} %bitcast.24, bf16[24,96,384]{2,1,0:T(8,128)(2,1)} %leg_ref.3, bf16[112,96]{1,0:T(8,128)(2,1)} %fusion.34.hot_ref, f32[112,1]{1,0:T(8,128)} %copy.23.weight_ref, ...), custom_call_target="tpu_custom_call" | custom-call | tf_op jit(solution)/shard_map/mix/pallas_call | solution.py:205
  116.1 2.3 %reshape.280 = bf16[24,16,7,256]{3,2,1,0:T(8,128)(2,1)S(1)} reshape(bf16[2,12,112,256]{3,2,1,0:T(8,128)(2,1)} %mix.3) | data formatting | bytes 2752512 | tf_op jit(solution)/shard_map/reshape | solution.py:304
  118.5 2.0 %copy.35 = bf16[24,16,7,256]{3,0,2,1:T(8,128)(2,1)} copy(bf16[24,16,7,256]{3,2,1,0:T(8,128)(2,1)S(1)} %reshape.280) | data formatting | bytes 2752512 | tf_op jit(solution)/shard_map/reshape | solution.py:304
  120.4 9.4 %all-to-all-done.1.refs_0_ = bf16[16,7,24,256]{3,2,1,0:T(8,128)(2,1)S(1)} async-done(((bf16[16,7,24,256]{3,2,1,0:T(8,128)(2,1)}), bf16[16,7,24,256]{3,2,1,0:T(8,128)(2,1)S(1)}, u32[]{:S(2)}, u32[]{:S(2)}) %all-to-all-start.1) | async-done | bytes 1376288 | tf_op jit(solution)/shard_map/all_to_all | solution.py:263
  129.9 4.7 %all-to-all-start.3 = ((bf16[16,7,24,256]{3,2,1,0:T(8,128)(2,1)}), bf16[16,7,24,256]{3,2,1,0:T(8,128)(2,1)S(1)}, u32[]{:S(2)}, u32[]{:S(2)}) async-start(bf16[16,7,24,256]{3,2,1,0:T(8,128)(2,1)} %bitcast.21), calls=%async_computation.3 | async-start | bytes 2752512 | tf_op jit(solution)/shard_map/all_to_all | solution.py:263
  134.7 0.3 fusion.40
  135.0 1.2 fusion.5
  136.2 2.0 %add_convert_fusion = bf16[15,96,768]{2,1,0:T(8,128)(2,1)} fusion(f32[96,768]{1,0:T(8,128)S(1)} %get-tuple-element.20, f32[15,768]{1,0:T(8,128)S(1)} %get-tuple-element.18, f32[96,768]{1,0:T(8,128)S(1)} %get-tuple-element.19, f32[15,768]{1,0:T(8,128)S(1)} %get-tuple-element.17), kind=kLoop, calls=%fused_computation | loop fusion | flops 4423680 | bytes 2893824 | tf_op jit(solution)/shard_map/convert_element_type | solution.py:73
  138.2 28.4 %all-to-all-done.3.refs_1_ = bf16[16,7,24,256]{3,2,1,0:T(8,128)(2,1)S(1)} async-done(((bf16[16,7,24,256]{3,2,1,0:T(8,128)(2,1)}), bf16[16,7,24,256]{3,2,1,0:T(8,128)(2,1)S(1)}, u32[]{:S(2)}, u32[]{:S(2)}) %all-to-all-start.3) | async-done | bytes 1376288 | tf_op jit(solution)/shard_map/all_to_all | solution.py:263
  166.6 1.1 copy-done.1
  167.7 9.6 %inverse.1 = bf16[7,1440,256]{2,1,0:T(8,128)(2,1)} custom-call(bf16[1440,768]{1,0:T(8,128)(2,1)} %bitcast.20, bf16[16,7,24,256]{3,2,1,0:T(8,128)(2,1)} %copy-done, bf16[16,7,24,256]{3,2,1,0:T(8,128)(2,1)} %copy-done.1), custom_call_target="tpu_custom_call" | custom-call | tf_op jit(solution)/shard_map/inverse/pallas_call | solution.py:241
  (31 shorter events, 0.4 us)
Async XLA Ops:
  16.4 40.1 %all-to-all-start = ((bf16[16,176,256]{2,1,0:T(8,128)(2,1)}), bf16[16,176,256]{2,1,0:T(8,128)(2,1)S(1)}, u32[]{:S(2)}, u32[]{:S(2)}) async-start(bf16[16,176,256]{2,1,0:T(8,128)(2,1)} %get-tuple-element.11), calls=%async_computation | async-start | bytes 2883584 | tf_op jit(solution)/shard_map/all_to_all | solution.py:263
  37.6 23.6 %copy-start.3 = (s32[16]{0:T(128)S(1)}, s32[16]{0:T(128)}, u32[]{:S(2)}) copy-start(s32[16]{0:T(128)} %count_ref.3) | copy-start | bytes 196
  37.6 24.1 %copy-start.5 = (f32[96]{0:T(128)S(1)}, f32[96]{0:T(128)}, u32[]{:S(2)}) copy-start(f32[96]{0:T(128)} %param.11) | copy-start | bytes 1156
  37.6 26.4 %copy-start.4 = (s32[384]{0:T(512)S(1)}, s32[384]{0:T(512)}, u32[]{:S(2)}) copy-start(s32[384]{0:T(512)} %param.9) | copy-start | bytes 4612
  56.4 36.7 %all-to-all-start.2 = ((bf16[16,7,24,256]{3,2,1,0:T(8,128)(2,1)}), bf16[16,7,24,256]{3,2,1,0:T(8,128)(2,1)S(1)}, u32[]{:S(2)}, u32[]{:S(2)}) async-start(bf16[16,7,24,256]{3,2,1,0:T(8,128)(2,1)} %get-tuple-element.14), calls=%async_computation.2 | async-start | bytes 2752512 | tf_op jit(solution)/shard_map/all_to_all | solution.py:263
  93.1 4.7 %copy-start.2 = (bf16[16,7,24,256]{3,2,1,0:T(8,128)(2,1)}, bf16[16,7,24,256]{3,2,1,0:T(8,128)(2,1)S(1)}, u32[]{:S(2)}) copy-start(bf16[16,7,24,256]{3,2,1,0:T(8,128)(2,1)S(1)} %all-to-all-done.2) | copy-start | bytes 4128772
  93.2 36.7 %all-to-all-start.1 = ((bf16[16,7,24,256]{3,2,1,0:T(8,128)(2,1)}), bf16[16,7,24,256]{3,2,1,0:T(8,128)(2,1)S(1)}, u32[]{:S(2)}, u32[]{:S(2)}) async-start(bf16[16,7,24,256]{3,2,1,0:T(8,128)(2,1)} %bitcast.22), calls=%async_computation.1 | async-start | bytes 2752512 | tf_op jit(solution)/shard_map/all_to_all | solution.py:263
  129.9 6.3 %copy-start = (bf16[16,7,24,256]{3,2,1,0:T(8,128)(2,1)}, bf16[16,7,24,256]{3,2,1,0:T(8,128)(2,1)S(1)}, u32[]{:S(2)}) copy-start(bf16[16,7,24,256]{3,2,1,0:T(8,128)(2,1)S(1)} %all-to-all-done.1.refs_0_) | copy-start | bytes 4128772
  129.9 36.7 %all-to-all-start.3 = ((bf16[16,7,24,256]{3,2,1,0:T(8,128)(2,1)}), bf16[16,7,24,256]{3,2,1,0:T(8,128)(2,1)S(1)}, u32[]{:S(2)}, u32[]{:S(2)}) async-start(bf16[16,7,24,256]{3,2,1,0:T(8,128)(2,1)} %bitcast.21), calls=%async_computation.3 | async-start | bytes 2752512 | tf_op jit(solution)/shard_map/all_to_all | solution.py:263
  166.6 1.1 copy-start.1

commit v3 on v2

--- a/solution.py
+++ b/solution.py
@@ -46,17 +46,9 @@
     return waves, sine
 
 
-def forward_parts(waves, sine, longitudes):
-    factor = 1.0 / math.sqrt(longitudes)
-    tiles = -(-longitudes // LANES)
-    low = sine & (waves == 0)
-    head = angle_of(waves[:, None], LANES * jnp.arange(tiles, dtype=jnp.int32)[None, :], longitudes)
+def forward_parts(waves, longitudes):
     step = angle_of(waves[:, None], jnp.arange(LANES, dtype=jnp.int32)[None, :], longitudes)
-    use_sine = (sine & (waves != 0))[:, None]
-    cos_head, sin_head = jnp.cos(head) * factor, jnp.sin(head) * factor
-    head_a = jnp.where(use_sine, -sin_head, cos_head)
-    head_b = jnp.where(use_sine, -cos_head, -sin_head)
-    return head_a, head_b, jnp.cos(step), jnp.sin(step), low.astype(F32)[:, None]
+    return jnp.cos(step), jnp.sin(step)
 
 
 def inverse_rows(waves, sine, longitudes):
@@ -74,30 +66,55 @@
     return table.reshape(longitudes, waves.shape[0])
 
 
+def sine_rows(shape, rows):
+    row = lax.broadcasted_iota(jnp.int32, shape, 0)
+    return lax.rem(row, jnp.int32(rows)) >= rows // 2
+
+
+def zero_wave(cos_ref, shape):
+    return jnp.broadcast_to(cos_ref[:, 1:2], shape) == 1.0
+
+
 def dft_kernel(
-    count_ref, x_ref, head_a, head_b, step_c, step_s, low_ref, out_ref, sum_ref,
-    table, stats, *, slots, devices, rows, with_stats,
+    count_ref, x_ref, cos_ref, sin_ref, out_ref, sum_ref, table, stats,
+    *, slots, devices, rows, with_stats,
 ):
     slot = pl.program_id(0)
     longitudes = x_ref.shape[0]
 
     @pl.when(slot == 0)
     def _():
-        total = jnp.zeros((devices * rows, 1), F32)
-        for i in range(head_a.shape[1]):
+        cosine, sine = cos_ref[...], sin_ref[...]
+        last = LANES - 1
+        turn_c = cosine[:, last:] * cosine[:, 1:2] - sine[:, last:] * sine[:, 1:2]
+        turn_s = sine[:, last:] * cosine[:, 1:2] + cosine[:, last:] * sine[:, 1:2]
+        turn_c = jnp.broadcast_to(turn_c, cosine.shape)
+        turn_s = jnp.broadcast_to(turn_s, cosine.shape)
+        factor = 1.0 / math.sqrt(longitudes)
+        use_sine = sine_rows(cosine.shape, rows) & jnp.logical_not(zero_wave(cos_ref, cosine.shape))
+        own = jnp.where(use_sine, -sine, cosine) * factor
+        other = jnp.where(use_sine, cosine, sine) * factor
+        total = jnp.zeros(cosine.shape, F32)
+        tiles = -(-longitudes // LANES)
+        for i in range(tiles):
             width = min(LANES, longitudes - LANES * i)
-            piece = (
-                head_a[:, i : i + 1] * step_c[:, :width] + head_b[:, i : i + 1] * step_s[:, :width]
-            ).astype(BF16)
-            table[:, LANES * i : LANES * i + width] = piece
-            total += jnp.sum(piece.astype(F32), axis=1, keepdims=True)
-        sum_ref[...] = jnp.broadcast_to(total, sum_ref.shape)
+            piece = own.astype(BF16)
+            table[:, LANES * i : LANES * i + width] = piece[:, :width]
+            kept = piece.astype(F32)
+            if width < LANES:
+                lane = lax.broadcasted_iota(jnp.int32, cosine.shape, 1)
+                kept = jnp.where(lane < width, kept, 0.0)
+            total += kept
+            if i + 1 < tiles:
+                own, other = own * turn_c - other * turn_s, other * turn_c + own * turn_s
+        sum_ref[...] = jnp.broadcast_to(jnp.sum(total, axis=1, keepdims=True), sum_ref.shape)
         stats[...] = jnp.zeros_like(stats)
 
     @pl.when(slot < slots)
     def _():
         acc = jnp.dot(table[...], x_ref[...], preferred_element_type=F32)
-        acc = acc - low_ref[...] * acc.astype(BF16).astype(F32)
+        low = sine_rows(acc.shape, rows) & zero_wave(cos_ref, acc.shape)
+        acc = jnp.where(low, acc - acc.astype(BF16).astype(F32), acc)
         for d in range(devices):
             out_ref[d] = acc[d * rows : (d + 1) * rows].astype(BF16)
 
@@ -269,11 +286,11 @@
 
     received, own_sums = [], []
     for h, size in enumerate(sizes):
-        waves, sine = rows_of[h]
+        waves, _ = rows_of[h]
         if h > 0:
             waves, _ = lax.optimization_barrier((waves, sums))
         out, sums = dft(
-            grid_values, lat_counts, forward_parts(waves, sine, longitudes), devices, 2 * size,
+            grid_values, lat_counts, forward_parts(waves, longitudes), devices, 2 * size,
             h == 0,
         )
         own_sums.append(lax.dynamic_slice(sums, (me * 2 * size, 0), (2 * size, 1))[:, 0])

time: 179 us -> 175 us (0.978)
  waiting for transfers between devices: 61.5 us -> 65.4 us
  other arithmetic: 12.4 us -> 8.73 us
  Pallas kernels: 55.8 us -> 52.9 us
    all_to_all x4, waiting for transfers between devices: 61.5 us -> 65.4 us  [body(): lax.all_to_all(a, 'lat', split_axis=0, concat_axis=0, tiled=True)]
    select_n x2 -> x0, other arithmetic: 3.54 us -> none  [forward_parts(): head_b = jnp.where(use_sine, -cos_head, -sin_head)]
    pallas_call x2, Pallas kernels: 20.9 us -> 18 us  [dft(): pl.pallas_call(functools.partial(dft_kernel, slots=slots, devices=devices...]
  transfers between devices with their start and end apart: 4 -> 4, of which waited for: 4 -> 4; matrix products, arithmetic and copies ran while one was open for 18% -> 17% of each run, Pallas kernels for 20% -> 20%
where the time goes in v3:
time: 175 us; the launch traced here: 173 us
  waiting for transfers between devices  65.4 us (37%)
  Pallas kernels  52.9 us (30%)
  local copies, waits for them, and re-layouts  24.8 us (14%)
  starting transfers between devices  21.1 us (12%)
  other arithmetic  8.73 us (5%)
    all_to_all x4, waiting for transfers between devices, body(): lax.all_to_all(a, 'lat', split_axis=0, concat_axis=0, tiled=True)  65.4 us
    pallas_call x2, Pallas kernels, mix(): pl.pallas_call(functools.partial(mix_kernel, size=size), grid=(size,), in...  25.2 us
    all_to_all x4, starting transfers between devices, body(): lax.all_to_all(a, 'lat', split_axis=0, concat_axis=0, tiled=True)  21.1 us
    pallas_call x2, Pallas kernels, dft(): pl.pallas_call(functools.partial(dft_kernel, slots=slots, devices=devices...  18 us
    pallas_call x1, Pallas kernels, final(): pl.pallas_call(final_kernel, grid=(slots,), in_specs=[pl.BlockSpec(table....  9.65 us
    reshape x4, local copies, waits for them, and re-layouts, body(): synthesis.reshape(2 * size, devices, slots, channels).transpose(1, 2, 0, 3)  8.57 us
    reshape x4, local copies, waits for them, and re-layouts, body(): received[h].reshape(devices * slots, 2, size, channels)  8.33 us
  transfers between devices with their start and end apart: 4, of which 4 were waited for; matrix products, arithmetic and copies ran while one was open for 17% of the time, Pallas kernels for 20%

profile of v3, /device:TPU:15, one launch (start us, length us, event | category | flops | bytes accessed | tf_op | source)
XLA Modules:
  0.0 173.1 jit_solution(7709111656366229577)
XLA Ops:
  0.0 0.8 reshape.224
  0.8 0.1 fusion.31
  0.8 0.1 reshape.225
  1.0 1.7 fusion.17
  2.7 9.3 %dft_stats.1 = (bf16[16,176,256]{2,1,0:T(8,128)(2,1)}, f32[384,128]{1,0:T(8,128)}) custom-call(s32[16]{0:T(128)} %count_ref.3, bf16[7,1440,256]{2,1,0:T(8,128)(2,1)} %x_ref.3, f32[384,128]{1,0:T(8,128)} %get-tuple-element.28.cos_ref, f32[384,128]{1,0:T(8,128)} %get-tuple-element.27.sin_ref), custom_call_target="tpu_custom_call" | custom-call | tf_op jit(solution)/shard_map/dft_stats/pallas_call | solution.py:155
  11.9 6.9 %all-to-all-start = ((bf16[16,176,256]{2,1,0:T(8,128)(2,1)}), bf16[16,176,256]{2,1,0:T(8,128)(2,1)S(1)}, u32[]{:S(2)}, u32[]{:S(2)}) async-start(bf16[16,176,256]{2,1,0:T(8,128)(2,1)} %get-tuple-element.11), calls=%async_computation | async-start | bytes 2883584 | tf_op jit(solution)/shard_map/all_to_all | solution.py:280
  18.8 0.1 reshape.226
  18.9 1.7 fusion.13
  20.6 8.8 %dft.1 = (bf16[16,7,24,256]{3,2,1,0:T(8,128)(2,1)}, f32[384,128]{1,0:T(8,128)}) custom-call(s32[16]{0:T(128)} %count_ref.3, bf16[7,1440,256]{2,1,0:T(8,128)(2,1)} %x_ref.3, f32[384,128]{1,0:T(8,128)} %get-tuple-element.22.cos_ref, f32[384,128]{1,0:T(8,128)} %get-tuple-element.21.sin_ref), custom_call_target="tpu_custom_call" | custom-call | tf_op jit(solution)/shard_map/dft/pallas_call | solution.py:155
  29.4 0.0 copy-start.4
  29.4 22.8 %all-to-all-done = bf16[16,176,256]{2,1,0:T(8,128)(2,1)S(1)} async-done(((bf16[16,176,256]{2,1,0:T(8,128)(2,1)}), bf16[16,176,256]{2,1,0:T(8,128)(2,1)S(1)}, u32[]{:S(2)}, u32[]{:S(2)}) %all-to-all-start) | async-done | bytes 1441824 | tf_op jit(solution)/shard_map/all_to_all | solution.py:280
  52.2 4.7 %all-to-all-start.2 = ((bf16[16,7,24,256]{3,2,1,0:T(8,128)(2,1)}), bf16[16,7,24,256]{3,2,1,0:T(8,128)(2,1)S(1)}, u32[]{:S(2)}, u32[]{:S(2)}) async-start(bf16[16,7,24,256]{3,2,1,0:T(8,128)(2,1)} %get-tuple-element.14), calls=%async_computation.2 | async-start | bytes 2752512 | tf_op jit(solution)/shard_map/all_to_all | solution.py:280
  56.9 0.1 iota_compare_fusion.2
  57.0 0.1 lt.72
  57.1 0.1 select_reduce_fusion.1
  57.2 0.1 iota_add_fusion
  57.3 0.1 add.86
  57.4 0.0 copy-done.5
  57.4 0.2 select_reduce_fusion
  57.6 0.7 copy.20.weight_ref
  58.3 1.4 dynamic-slice_reduce_fusion.1.sums_ref
  59.7 0.6 fusion.32
  60.3 0.7 fusion.22.hot_ref
  61.1 1.2 slice.28
  62.2 2.3 %reshape.227 = bf16[112,2,12,256]{3,2,1,0:T(8,128)(2,1)S(1)} reshape(bf16[16,168,256]{2,1,0:T(8,128)(2,1)} %slice.28) | data formatting | bytes 2752512 | tf_op jit(solution)/shard_map/reshape | solution.py:315
  64.5 1.8 %copy.33 = bf16[112,2,12,256]{3,0,2,1:T(8,128)(2,1)} copy(bf16[112,2,12,256]{3,2,1,0:T(8,128)(2,1)S(1)} %reshape.227) | data formatting | bytes 2752512 | tf_op jit(solution)/shard_map/reshape | solution.py:315
  66.4 0.6 pad_maximum_fusion.moment_ref
  67.0 12.6 %mix.2 = bf16[2,12,112,256]{3,2,1,0:T(8,128)(2,1)} custom-call(s32[12]{0:T(128)} %get-tuple-element.24.wave_ref, f32[24]{0:T(128)} %dynamic-slice_reduce_fusion.1.sums_ref, bf16[2,12,112,256]{3,2,1,0:T(8,128)(2,1)} %bitcast.23, bf16[24,96,384]{2,1,0:T(8,128)(2,1)} %leg_ref.3, bf16[112,96]{1,0:T(8,128)(2,1)} %fusion.22.hot_ref, f32[112,1]{1,0:T(8,128)} %copy.20.weight_ref, ...), custom_call_target="tpu_custom_call" | custom-call | tf_op jit(solution)/shard_map/mix/pallas_call | solution.py:222
  79.6 2.3 %reshape.228 = bf16[24,16,7,256]{3,2,1,0:T(8,128)(2,1)S(1)} reshape(bf16[2,12,112,256]{3,2,1,0:T(8,128)(2,1)} %mix.2) | data formatting | bytes 2752512 | tf_op jit(solution)/shard_map/reshape | solution.py:321
  82.0 1.9 %copy.32 = bf16[24,16,7,256]{3,0,2,1:T(8,128)(2,1)} copy(bf16[24,16,7,256]{3,2,1,0:T(8,128)(2,1)S(1)} %reshape.228) | data formatting | bytes 2752512 | tf_op jit(solution)/shard_map/reshape | solution.py:321
  83.9 5.0 %all-to-all-done.2 = bf16[16,7,24,256]{3,2,1,0:T(8,128)(2,1)S(1)} async-done(((bf16[16,7,24,256]{3,2,1,0:T(8,128)(2,1)}), bf16[16,7,24,256]{3,2,1,0:T(8,128)(2,1)S(1)}, u32[]{:S(2)}, u32[]{:S(2)}) %all-to-all-start.2) | async-done | bytes 1376288 | tf_op jit(solution)/shard_map/all_to_all | solution.py:280
  88.9 4.7 %all-to-all-start.1 = ((bf16[16,7,24,256]{3,2,1,0:T(8,128)(2,1)}), bf16[16,7,24,256]{3,2,1,0:T(8,128)(2,1)S(1)}, u32[]{:S(2)}, u32[]{:S(2)}) async-start(bf16[16,7,24,256]{3,2,1,0:T(8,128)(2,1)} %bitcast.22), calls=%async_computation.1 | async-start | bytes 2752512 | tf_op jit(solution)/shard_map/all_to_all | solution.py:280
  93.6 1.4 dynamic-slice_reduce_fusion.sums_ref
  95.1 2.3 %reshape.231 = bf16[112,2,12,256]{3,2,1,0:T(8,128)(2,1)S(1)} reshape(bf16[16,7,24,256]{3,2,1,0:T(8,128)(2,1)} %copy-done.2) | data formatting | bytes 2752512 | tf_op jit(solution)/shard_map/reshape | solution.py:315
  97.4 1.9 %copy.30 = bf16[112,2,12,256]{3,0,2,1:T(8,128)(2,1)} copy(bf16[112,2,12,256]{3,2,1,0:T(8,128)(2,1)S(1)} %reshape.231) | data formatting | bytes 2752512 | tf_op jit(solution)/shard_map/reshape | solution.py:315
  99.2 12.6 %mix.3 = bf16[2,12,112,256]{3,2,1,0:T(8,128)(2,1)} custom-call(s32[12]{0:T(128)} %get-tuple-element.23.wave_ref, f32[24]{0:T(128)} %dynamic-slice_reduce_fusion.sums_ref, bf16[2,12,112,256]{3,2,1,0:T(8,128)(2,1)} %bitcast.24, bf16[24,96,384]{2,1,0:T(8,128)(2,1)} %leg_ref.3, bf16[112,96]{1,0:T(8,128)(2,1)} %fusion.22.hot_ref, f32[112,1]{1,0:T(8,128)} %copy.20.weight_ref, ...), custom_call_target="tpu_custom_call" | custom-call | tf_op jit(solution)/shard_map/mix/pallas_call | solution.py:222
  111.9 2.3 %reshape.230 = bf16[24,16,7,256]{3,2,1,0:T(8,128)(2,1)S(1)} reshape(bf16[2,12,112,256]{3,2,1,0:T(8,128)(2,1)} %mix.3) | data formatting | bytes 2752512 | tf_op jit(solution)/shard_map/reshape | solution.py:321
  114.2 2.0 %copy.31 = bf16[24,16,7,256]{3,0,2,1:T(8,128)(2,1)} copy(bf16[24,16,7,256]{3,2,1,0:T(8,128)(2,1)S(1)} %reshape.230) | data formatting | bytes 2752512 | tf_op jit(solution)/shard_map/reshape | solution.py:321
  116.2 9.4 %all-to-all-done.1.refs_0_ = bf16[16,7,24,256]{3,2,1,0:T(8,128)(2,1)S(1)} async-done(((bf16[16,7,24,256]{3,2,1,0:T(8,128)(2,1)}), bf16[16,7,24,256]{3,2,1,0:T(8,128)(2,1)S(1)}, u32[]{:S(2)}, u32[]{:S(2)}) %all-to-all-start.1) | async-done | bytes 1376288 | tf_op jit(solution)/shard_map/all_to_all | solution.py:280
  125.6 4.7 %all-to-all-start.3 = ((bf16[16,7,24,256]{3,2,1,0:T(8,128)(2,1)}), bf16[16,7,24,256]{3,2,1,0:T(8,128)(2,1)S(1)}, u32[]{:S(2)}, u32[]{:S(2)}) async-start(bf16[16,7,24,256]{3,2,1,0:T(8,128)(2,1)} %bitcast.21), calls=%async_computation.3 | async-start | bytes 2752512 | tf_op jit(solution)/shard_map/all_to_all | solution.py:280
  130.4 0.1 broadcast_in_dim.38
  130.4 0.1 reshape.223
  130.6 0.3 fusion.28
  130.9 1.2 fusion.5
  132.2 2.0 %add_convert_fusion = bf16[15,96,768]{2,1,0:T(8,128)(2,1)} fusion(f32[96,768]{1,0:T(8,128)S(1)} %get-tuple-element.20, f32[15,768]{1,0:T(8,128)S(1)} %get-tuple-element.18, f32[96,768]{1,0:T(8,128)S(1)} %get-tuple-element.19, f32[15,768]{1,0:T(8,128)S(1)} %get-tuple-element.17), kind=kLoop, calls=%fused_computation | loop fusion | flops 4423680 | bytes 2893824 | tf_op jit(solution)/shard_map/convert_element_type | solution.py:65
  134.1 28.2 %all-to-all-done.3.refs_1_ = bf16[16,7,24,256]{3,2,1,0:T(8,128)(2,1)S(1)} async-done(((bf16[16,7,24,256]{3,2,1,0:T(8,128)(2,1)}), bf16[16,7,24,256]{3,2,1,0:T(8,128)(2,1)S(1)}, u32[]{:S(2)}, u32[]{:S(2)}) %all-to-all-start.3) | async-done | bytes 1376288 | tf_op jit(solution)/shard_map/all_to_all | solution.py:280
  162.3 1.1 copy-done.1
  163.4 9.6 %inverse.1 = bf16[7,1440,256]{2,1,0:T(8,128)(2,1)} custom-call(bf16[1440,768]{1,0:T(8,128)(2,1)} %bitcast.20, bf16[16,7,24,256]{3,2,1,0:T(8,128)(2,1)} %copy-done, bf16[16,7,24,256]{3,2,1,0:T(8,128)(2,1)} %copy-done.1), custom_call_target="tpu_custom_call" | custom-call | tf_op jit(solution)/shard_map/inverse/pallas_call | solution.py:258
  (22 shorter events, 0.1 us)
Async XLA Ops:
  11.9 40.2 %all-to-all-start = ((bf16[16,176,256]{2,1,0:T(8,128)(2,1)}), bf16[16,176,256]{2,1,0:T(8,128)(2,1)S(1)}, u32[]{:S(2)}, u32[]{:S(2)}) async-start(bf16[16,176,256]{2,1,0:T(8,128)(2,1)} %get-tuple-element.11), calls=%async_computation | async-start | bytes 2883584 | tf_op jit(solution)/shard_map/all_to_all | solution.py:280
  29.4 27.5 %copy-start.3 = (s32[16]{0:T(128)S(1)}, s32[16]{0:T(128)}, u32[]{:S(2)}) copy-start(s32[16]{0:T(128)} %count_ref.3) | copy-start | bytes 196
  29.4 28.0 %copy-start.5 = (f32[96]{0:T(128)S(1)}, f32[96]{0:T(128)}, u32[]{:S(2)}) copy-start(f32[96]{0:T(128)} %param.11) | copy-start | bytes 1156
  29.4 30.3 %copy-start.4 = (s32[384]{0:T(512)S(1)}, s32[384]{0:T(512)}, u32[]{:S(2)}) copy-start(s32[384]{0:T(512)} %param.9) | copy-start | bytes 4612
  52.2 36.7 %all-to-all-start.2 = ((bf16[16,7,24,256]{3,2,1,0:T(8,128)(2,1)}), bf16[16,7,24,256]{3,2,1,0:T(8,128)(2,1)S(1)}, u32[]{:S(2)}, u32[]{:S(2)}) async-start(bf16[16,7,24,256]{3,2,1,0:T(8,128)(2,1)} %get-tuple-element.14), calls=%async_computation.2 | async-start | bytes 2752512 | tf_op jit(solution)/shard_map/all_to_all | solution.py:280
  88.9 4.7 %copy-start.2 = (bf16[16,7,24,256]{3,2,1,0:T(8,128)(2,1)}, bf16[16,7,24,256]{3,2,1,0:T(8,128)(2,1)S(1)}, u32[]{:S(2)}) copy-start(bf16[16,7,24,256]{3,2,1,0:T(8,128)(2,1)S(1)} %all-to-all-done.2) | copy-start | bytes 4128772
  88.9 36.7 %all-to-all-start.1 = ((bf16[16,7,24,256]{3,2,1,0:T(8,128)(2,1)}), bf16[16,7,24,256]{3,2,1,0:T(8,128)(2,1)S(1)}, u32[]{:S(2)}, u32[]{:S(2)}) async-start(bf16[16,7,24,256]{3,2,1,0:T(8,128)(2,1)} %bitcast.22), calls=%async_computation.1 | async-start | bytes 2752512 | tf_op jit(solution)/shard_map/all_to_all | solution.py:280
  125.6 6.5 %copy-start = (bf16[16,7,24,256]{3,2,1,0:T(8,128)(2,1)}, bf16[16,7,24,256]{3,2,1,0:T(8,128)(2,1)S(1)}, u32[]{:S(2)}) copy-start(bf16[16,7,24,256]{3,2,1,0:T(8,128)(2,1)S(1)} %all-to-all-done.1.refs_0_) | copy-start | bytes 4128772
  125.6 36.7 %all-to-all-start.3 = ((bf16[16,7,24,256]{3,2,1,0:T(8,128)(2,1)}), bf16[16,7,24,256]{3,2,1,0:T(8,128)(2,1)S(1)}, u32[]{:S(2)}, u32[]{:S(2)}) async-start(bf16[16,7,24,256]{3,2,1,0:T(8,128)(2,1)} %bitcast.21), calls=%async_computation.3 | async-start | bytes 2752512 | tf_op jit(solution)/shard_map/all_to_all | solution.py:280
  162.3 1.1 copy-start.1

commit v4 on v3

--- a/solution.py
+++ b/solution.py
@@ -239,35 +239,34 @@
     )(waves, sums, raw, legendre, hot, weight, moments, gain, mixer)
 
 
-def final_kernel(table_ref, *refs):
-    *parts, out_ref, gathered = refs
-    at = 0
-    for part in parts:
-        devices, rows, _ = part.shape
-        for d in range(devices):
-            gathered[at : at + rows] = part[d]
-            at += rows
-    out_ref[...] = jnp.dot(
-        table_ref[...], gathered[...], preferred_element_type=F32
-    ).astype(BF16)
-
-
-def final(table, parts):
+def inverse_kernel(table_ref, part_ref, *refs):
+    *before, out_ref, gathered = refs
+    devices, rows, _ = part_ref.shape
+    for d in range(devices):
+        gathered[d * rows : (d + 1) * rows] = part_ref[d]
+    result = jnp.dot(table_ref[...], gathered[...], preferred_element_type=F32)
+    if before:
+        result = result + before[0][...].astype(F32)
+    out_ref[...] = result.astype(BF16)
+
+
+def inverse(table, part, before=()):
     longitudes, total = table.shape
-    devices, slots, _, channels = parts[0].shape
+    devices, slots, rows, channels = part.shape
+    grid_block = pl.BlockSpec((None, longitudes, channels), lambda s: (s, 0, 0))
     return pl.pallas_call(
-        final_kernel,
+        inverse_kernel,
         grid=(slots,),
-        in_specs=[pl.BlockSpec(table.shape, lambda s: (0, 0))]
-        + [
-            pl.BlockSpec((devices, None, p.shape[2], channels), lambda s: (0, s, 0, 0))
-            for p in parts
-        ],
-        out_specs=pl.BlockSpec((None, longitudes, channels), lambda s: (s, 0, 0)),
+        in_specs=[
+            pl.BlockSpec(table.shape, lambda s: (0, 0)),
+            pl.BlockSpec((devices, None, rows, channels), lambda s: (0, s, 0, 0)),
+        ]
+        + [grid_block] * len(before),
+        out_specs=grid_block,
         out_shape=jax.ShapeDtypeStruct((slots, longitudes, channels), BF16),
         scratch_shapes=[pltpu.VMEM((total, channels), BF16)],
         name="inverse",
-    )(table, *parts)
+    )(table, part, *before)
 
 
 def body(
@@ -321,9 +320,10 @@
         outgoing = synthesis.reshape(2 * size, devices, slots, channels).transpose(1, 2, 0, 3)
         returned.append(exchange(outgoing))
 
-    waves = jnp.concatenate([w for w, _ in rows_of])
-    sine = jnp.concatenate([s for _, s in rows_of])
-    return final(inverse_rows(waves, sine, longitudes), returned)
+    result = ()
+    for (waves, sine), part in zip(rows_of, returned):
+        result = (inverse(inverse_rows(waves, sine, longitudes), part, result),)
+    return result[0]
 
 
 def solution(mesh):

time: 175 us -> 174 us (level)
  Pallas kernels: 52.9 us -> 60.3 us
  waiting for transfers between devices: 65.4 us -> 58.9 us
  local copies, waits for them, and re-layouts: 24.8 us -> 22.8 us
    pallas_call x1 -> x2, Pallas kernels: 9.65 us -> 17.1 us  [inverse(): pl.pallas_call(inverse_kernel, grid=(slots,), in_specs=[pl.BlockSpec(tabl...]
    all_to_all x4, waiting for transfers between devices: 65.4 us -> 58.9 us  [body(): lax.all_to_all(a, 'lat', split_axis=0, concat_axis=0, tiled=True)]
    reshape x4, local copies, waits for them, and re-layouts: 8.33 us -> 6.33 us  [body(): received[h].reshape(devices * slots, 2, size, channels)]
  transfers between devices with their start and end apart: 4 -> 4, of which waited for: 4 -> 4; matrix products, arithmetic and copies ran while one was open for 17% -> 16% of each run, Pallas kernels for 20% -> 24%
where the time goes in v4:
time: 174 us; the launch traced here: 173 us
  Pallas kernels  60.3 us (35%)
  waiting for transfers between devices  58.9 us (34%)
  local copies, waits for them, and re-layouts  22.8 us (13%)
  starting transfers between devices  21.1 us (12%)
  other arithmetic  9.5 us (5%)
    all_to_all x4, waiting for transfers between devices, body(): lax.all_to_all(a, 'lat', split_axis=0, concat_axis=0, tiled=True)  58.9 us
    pallas_call x2, Pallas kernels, mix(): pl.pallas_call(functools.partial(mix_kernel, size=size), grid=(size,), in...  25.2 us
    all_to_all x4, starting transfers between devices, body(): lax.all_to_all(a, 'lat', split_axis=0, concat_axis=0, tiled=True)  21.1 us
    pallas_call x2, Pallas kernels, dft(): pl.pallas_call(functools.partial(dft_kernel, slots=slots, devices=devices...  18 us
    pallas_call x2, Pallas kernels, inverse(): pl.pallas_call(inverse_kernel, grid=(slots,), in_specs=[pl.BlockSpec(tabl...  17.1 us
    reshape x4, local copies, waits for them, and re-layouts, body(): synthesis.reshape(2 * size, devices, slots, channels).transpose(1, 2, 0, 3)  8.57 us
    reshape x4, local copies, waits for them, and re-layouts, body(): received[h].reshape(devices * slots, 2, size, channels)  6.33 us
  transfers between devices with their start and end apart: 4, of which 4 were waited for; matrix products, arithmetic and copies ran while one was open for 16% of the time, Pallas kernels for 24%

profile of v4, /device:TPU:15, one launch (start us, length us, event | category | flops | bytes accessed | tf_op | source)
XLA Modules:
  0.0 172.7 jit_solution(9816936985145566929)
XLA Ops:
  0.0 0.8 reshape.389
  0.8 0.1 mul.298
  1.0 1.7 fusion.10
  2.7 9.3 %dft_stats.1 = (bf16[16,176,256]{2,1,0:T(8,128)(2,1)}, f32[384,128]{1,0:T(8,128)}) custom-call(s32[16]{0:T(128)} %count_ref.3, bf16[7,1440,256]{2,1,0:T(8,128)(2,1)} %x_ref.3, f32[384,128]{1,0:T(8,128)} %get-tuple-element.30.cos_ref, f32[384,128]{1,0:T(8,128)} %get-tuple-element.29.sin_ref), custom_call_target="tpu_custom_call" | custom-call | tf_op jit(solution)/shard_map/dft_stats/pallas_call | solution.py:155
  11.9 6.9 %all-to-all-start.1 = ((bf16[16,176,256]{2,1,0:T(8,128)(2,1)}), bf16[16,176,256]{2,1,0:T(8,128)(2,1)S(1)}, u32[]{:S(2)}, u32[]{:S(2)}) async-start(bf16[16,176,256]{2,1,0:T(8,128)(2,1)} %get-tuple-element.14), calls=%async_computation.1 | async-start | bytes 2883584 | tf_op jit(solution)/shard_map/all_to_all | solution.py:279
  18.9 0.1 mul.279
  19.0 1.7 fusion.6
  20.7 8.8 %dft.1 = (bf16[16,7,24,256]{3,2,1,0:T(8,128)(2,1)}, f32[384,128]{1,0:T(8,128)}) custom-call(s32[16]{0:T(128)} %count_ref.3, bf16[7,1440,256]{2,1,0:T(8,128)(2,1)} %x_ref.3, f32[384,128]{1,0:T(8,128)} %get-tuple-element.28.cos_ref, f32[384,128]{1,0:T(8,128)} %get-tuple-element.27.sin_ref), custom_call_target="tpu_custom_call" | custom-call | tf_op jit(solution)/shard_map/dft/pallas_call | solution.py:155
  29.5 22.8 %all-to-all-done.1 = bf16[16,176,256]{2,1,0:T(8,128)(2,1)S(1)} async-done(((bf16[16,176,256]{2,1,0:T(8,128)(2,1)}), bf16[16,176,256]{2,1,0:T(8,128)(2,1)S(1)}, u32[]{:S(2)}, u32[]{:S(2)}) %all-to-all-start.1) | async-done | bytes 1441824 | tf_op jit(solution)/shard_map/all_to_all | solution.py:279
  52.2 4.7 %all-to-all-start = ((bf16[16,7,24,256]{3,2,1,0:T(8,128)(2,1)}), bf16[16,7,24,256]{3,2,1,0:T(8,128)(2,1)S(1)}, u32[]{:S(2)}, u32[]{:S(2)}) async-start(bf16[16,7,24,256]{3,2,1,0:T(8,128)(2,1)} %get-tuple-element.13), calls=%async_computation | async-start | bytes 2752512 | tf_op jit(solution)/shard_map/all_to_all | solution.py:279
  57.0 0.1 iota_compare_fusion.2
  57.0 0.1 lt.82
  57.1 0.1 select_reduce_fusion.1
  57.3 0.1 iota_add_fusion
  57.3 0.1 add.116
  57.4 0.2 select_reduce_fusion
  57.6 0.8 copy.20.weight_ref
  58.4 1.3 dynamic-slice_reduce_fusion.sums_ref
  59.7 0.7 fusion.45
  60.4 0.7 fusion.29.hot_ref
  61.1 1.2 slice.31
  62.3 2.3 %reshape.392 = bf16[112,2,12,256]{3,2,1,0:T(8,128)(2,1)S(1)} reshape(bf16[16,168,256]{2,1,0:T(8,128)(2,1)} %slice.31) | data formatting | bytes 2752512 | tf_op jit(solution)/shard_map/reshape | solution.py:314
  64.6 1.8 %copy.32 = bf16[112,2,12,256]{3,0,2,1:T(8,128)(2,1)} copy(bf16[112,2,12,256]{3,2,1,0:T(8,128)(2,1)S(1)} %reshape.392) | data formatting | bytes 2752512 | tf_op jit(solution)/shard_map/reshape | solution.py:314
  66.5 0.6 pad_maximum_fusion.moment_ref
  67.1 12.6 %mix.3 = bf16[2,12,112,256]{3,2,1,0:T(8,128)(2,1)} custom-call(s32[12]{0:T(128)} %get-tuple-element.21.wave_ref, f32[24]{0:T(128)} %dynamic-slice_reduce_fusion.sums_ref, bf16[2,12,112,256]{3,2,1,0:T(8,128)(2,1)} %bitcast.22, bf16[24,96,384]{2,1,0:T(8,128)(2,1)} %leg_ref.3, bf16[112,96]{1,0:T(8,128)(2,1)} %fusion.29.hot_ref, f32[112,1]{1,0:T(8,128)} %copy.20.weight_ref, ...), custom_call_target="tpu_custom_call" | custom-call | tf_op jit(solution)/shard_map/mix/pallas_call | solution.py:222
  79.7 2.3 %reshape.393 = bf16[24,16,7,256]{3,2,1,0:T(8,128)(2,1)S(1)} reshape(bf16[2,12,112,256]{3,2,1,0:T(8,128)(2,1)} %mix.3) | data formatting | bytes 2752512 | tf_op jit(solution)/shard_map/reshape | solution.py:320
  82.0 2.0 %copy.31 = bf16[24,16,7,256]{3,0,2,1:T(8,128)(2,1)} copy(bf16[24,16,7,256]{3,2,1,0:T(8,128)(2,1)S(1)} %reshape.393) | data formatting | bytes 2752512 | tf_op jit(solution)/shard_map/reshape | solution.py:320
  84.0 4.9 %all-to-all-done = bf16[16,7,24,256]{3,2,1,0:T(8,128)(2,1)S(1)} async-done(((bf16[16,7,24,256]{3,2,1,0:T(8,128)(2,1)}), bf16[16,7,24,256]{3,2,1,0:T(8,128)(2,1)S(1)}, u32[]{:S(2)}, u32[]{:S(2)}) %all-to-all-start) | async-done | bytes 1376288 | tf_op jit(solution)/shard_map/all_to_all | solution.py:279
  88.9 4.7 %all-to-all-start.3 = ((bf16[16,7,24,256]{3,2,1,0:T(8,128)(2,1)}), bf16[16,7,24,256]{3,2,1,0:T(8,128)(2,1)}, u32[]{:S(2)}, u32[]{:S(2)}) async-start(bf16[16,7,24,256]{3,2,1,0:T(8,128)(2,1)} %bitcast.21), calls=%async_computation.3 | async-start | bytes 2752512 | tf_op jit(solution)/shard_map/all_to_all | solution.py:279
  93.7 1.3 dynamic-slice_reduce_fusion.1.sums_ref
  95.0 0.3 reshape.394
  95.3 1.8 %copy.30 = bf16[112,2,12,256]{3,0,2,1:T(8,128)(2,1)} copy(bf16[112,2,12,256]{3,2,1,0:T(8,128)(2,1)S(1)} %reshape.394) | data formatting | bytes 2752512 | tf_op jit(solution)/shard_map/reshape | solution.py:314
  97.2 12.6 %mix.2 = bf16[2,12,112,256]{3,2,1,0:T(8,128)(2,1)} custom-call(s32[12]{0:T(128)} %get-tuple-element.22.wave_ref, f32[24]{0:T(128)} %dynamic-slice_reduce_fusion.1.sums_ref, bf16[2,12,112,256]{3,2,1,0:T(8,128)(2,1)} %bitcast.23, bf16[24,96,384]{2,1,0:T(8,128)(2,1)} %leg_ref.3, bf16[112,96]{1,0:T(8,128)(2,1)} %fusion.29.hot_ref, f32[112,1]{1,0:T(8,128)} %copy.20.weight_ref, ...), custom_call_target="tpu_custom_call" | custom-call | tf_op jit(solution)/shard_map/mix/pallas_call | solution.py:222
  109.8 2.3 %reshape.391 = bf16[24,16,7,256]{3,2,1,0:T(8,128)(2,1)S(1)} reshape(bf16[2,12,112,256]{3,2,1,0:T(8,128)(2,1)} %mix.2) | data formatting | bytes 2752512 | tf_op jit(solution)/shard_map/reshape | solution.py:320
  112.2 1.9 %copy.33 = bf16[24,16,7,256]{3,0,2,1:T(8,128)(2,1)} copy(bf16[24,16,7,256]{3,2,1,0:T(8,128)(2,1)S(1)} %reshape.391) | data formatting | bytes 2752512 | tf_op jit(solution)/shard_map/reshape | solution.py:320
  114.1 11.6 %all-to-all-done.3.part_ref = bf16[16,7,24,256]{3,2,1,0:T(8,128)(2,1)} async-done(((bf16[16,7,24,256]{3,2,1,0:T(8,128)(2,1)}), bf16[16,7,24,256]{3,2,1,0:T(8,128)(2,1)}, u32[]{:S(2)}, u32[]{:S(2)}) %all-to-all-start.3) | async-done | bytes 1376288 | tf_op jit(solution)/shard_map/all_to_all | solution.py:279
  125.7 4.7 %all-to-all-start.2 = ((bf16[16,7,24,256]{3,2,1,0:T(8,128)(2,1)}), bf16[16,7,24,256]{3,2,1,0:T(8,128)(2,1)S(1)}, u32[]{:S(2)}, u32[]{:S(2)}) async-start(bf16[16,7,24,256]{3,2,1,0:T(8,128)(2,1)} %bitcast.20), calls=%async_computation.2 | async-start | bytes 2752512 | tf_op jit(solution)/shard_map/all_to_all | solution.py:279
  130.5 0.1 broadcast_in_dim.112
  130.6 0.1 broadcast_in_dim.113
  130.7 0.3 fusion.41
  131.0 0.6 fusion.25
  131.6 0.6 fusion.21
  132.2 1.4 add_convert_fusion
  133.6 1.3 add_convert_fusion.1
  134.9 8.0 %inverse.2.refs_0_ = bf16[7,1440,256]{2,1,0:T(8,128)(2,1)} custom-call(bf16[1440,384]{1,0:T(8,128)(2,1)} %bitcast.24, bf16[16,7,24,256]{3,2,1,0:T(8,128)(2,1)} %all-to-all-done.3.part_ref), custom_call_target="tpu_custom_call" | custom-call | tf_op jit(solution)/shard_map/inverse/pallas_call | solution.py:257
  142.9 19.5 %all-to-all-done.2.part_ref = bf16[16,7,24,256]{3,2,1,0:T(8,128)(2,1)S(1)} async-done(((bf16[16,7,24,256]{3,2,1,0:T(8,128)(2,1)}), bf16[16,7,24,256]{3,2,1,0:T(8,128)(2,1)S(1)}, u32[]{:S(2)}, u32[]{:S(2)}) %all-to-all-start.2) | async-done | bytes 1376288 | tf_op jit(solution)/shard_map/all_to_all | solution.py:279
  162.4 1.1 copy-done
  163.6 9.1 %inverse.3 = bf16[7,1440,256]{2,1,0:T(8,128)(2,1)} custom-call(bf16[1440,384]{1,0:T(8,128)(2,1)} %bitcast.25, bf16[16,7,24,256]{3,2,1,0:T(8,128)(2,1)} %copy-done, bf16[7,1440,256]{2,1,0:T(8,128)(2,1)} %inverse.2.refs_0_), custom_call_target="tpu_custom_call" | custom-call | tf_op jit(solution)/shard_map/inverse/pallas_call | solution.py:257
  (17 shorter events, 0.2 us)
Async XLA Ops:
  11.9 40.3 %all-to-all-start.1 = ((bf16[16,176,256]{2,1,0:T(8,128)(2,1)}), bf16[16,176,256]{2,1,0:T(8,128)(2,1)S(1)}, u32[]{:S(2)}, u32[]{:S(2)}) async-start(bf16[16,176,256]{2,1,0:T(8,128)(2,1)} %get-tuple-element.14), calls=%async_computation.1 | async-start | bytes 2883584 | tf_op jit(solution)/shard_map/all_to_all | solution.py:279
  29.4 27.5 %copy-start.1 = (s32[16]{0:T(128)S(1)}, s32[16]{0:T(128)}, u32[]{:S(2)}) copy-start(s32[16]{0:T(128)} %count_ref.3) | copy-start | bytes 196
  29.4 28.0 %copy-start.3 = (f32[96]{0:T(128)S(1)}, f32[96]{0:T(128)}, u32[]{:S(2)}) copy-start(f32[96]{0:T(128)} %param.11) | copy-start | bytes 1156
  29.4 30.3 %copy-start.2 = (s32[384]{0:T(512)S(1)}, s32[384]{0:T(512)}, u32[]{:S(2)}) copy-start(s32[384]{0:T(512)} %param.9) | copy-start | bytes 4612
  52.2 36.7 %all-to-all-start = ((bf16[16,7,24,256]{3,2,1,0:T(8,128)(2,1)}), bf16[16,7,24,256]{3,2,1,0:T(8,128)(2,1)S(1)}, u32[]{:S(2)}, u32[]{:S(2)}) async-start(bf16[16,7,24,256]{3,2,1,0:T(8,128)(2,1)} %get-tuple-element.13), calls=%async_computation | async-start | bytes 2752512 | tf_op jit(solution)/shard_map/all_to_all | solution.py:279
  88.9 36.8 %all-to-all-start.3 = ((bf16[16,7,24,256]{3,2,1,0:T(8,128)(2,1)}), bf16[16,7,24,256]{3,2,1,0:T(8,128)(2,1)}, u32[]{:S(2)}, u32[]{:S(2)}) async-start(bf16[16,7,24,256]{3,2,1,0:T(8,128)(2,1)} %bitcast.21), calls=%async_computation.3 | async-start | bytes 2752512 | tf_op jit(solution)/shard_map/all_to_all | solution.py:279
  125.7 36.7 %all-to-all-start.2 = ((bf16[16,7,24,256]{3,2,1,0:T(8,128)(2,1)}), bf16[16,7,24,256]{3,2,1,0:T(8,128)(2,1)S(1)}, u32[]{:S(2)}, u32[]{:S(2)}) async-start(bf16[16,7,24,256]{3,2,1,0:T(8,128)(2,1)} %bitcast.20), calls=%async_computation.2 | async-start | bytes 2752512 | tf_op jit(solution)/shard_map/all_to_all | solution.py:279
  162.4 1.1 copy-start
